TPU v7x, 32 devices: a whole 2x2x4 slice. The times are simulated.
32 devices in a mesh: tm: 8 (over z, y), space: 4 (over x, core).
Axes of the slice: x: 2, y: 2, z: 4, core: 2. Of those that a mesh axis runs over, the one named last changes fastest.
Arguments:
- initial: float32 [8, 128, 128], P('space'), may hold values from -6 to 6
- start_guess: float32 [8, 8, 128, 128], P('tm', 'space'), may hold values from -6 to 6
- forcing: float32 [8, 5, 8, 128, 128], P('tm', None, 'space'), may hold values from -6 to 6
- step_size: float32 [8], P('tm'), may hold values from 0.06 to 0.16
Outputs:
- fine_values: float32 [8, 5, 8, 128, 128], P('tm', None, 'space')
All inputs are finite; a program needn't handle non-finite values.
Results may differ from a plain program's by a relative error of at most 0.0001.
Values sent between devices are 32-bit elements; how exact they have to be, the bound alone decides.
No kernel may reach another device: no remote copies, remote signals or barrier semaphores. Data moves between devices by JAX's collectives and lax.ppermute only.
A program may use at most 64 MiB of HBM per device.

v0:
```python
import math

import jax
import jax.numpy as jnp
import numpy as np
from jax import lax
from jax.sharding import PartitionSpec as P

ITERS = 2


def with_halo(block, sides, width):
    for axis, dim in sides:
        count = lax.axis_size(axis)
        forward = [(i, i + 1) for i in range(count - 1)]
        backward = [(target, source) for source, target in forward]
        low = lax.ppermute(
            lax.slice_in_dim(block, block.shape[dim] - width, None, axis=dim), axis, forward
        )
        high = lax.ppermute(lax.slice_in_dim(block, 0, width, axis=dim), axis, backward)
        block = jnp.concatenate([low, block, high], axis=dim)
    return block


def shifted(value, axis, steps):
    count = lax.axis_size(axis)
    first, last = (max(0, -steps), min(count, count - steps))
    return lax.ppermute(value, axis, [(source, source + steps) for source in range(first, last)])


def prefix(part, axis, combine, identity):
    place = lax.axis_index(axis)
    gathered = jax.tree.map(lambda a: lax.all_gather(a, axis), part)
    state = jax.tree.map(lambda a, e: jnp.zeros_like(a) + jnp.asarray(e, a.dtype), part, identity)

    def one(step, state):
        return combine(
            state, jax.tree.map(lambda a: lax.dynamic_index_in_dim(a, step, 0, False), gathered)
        )

    return lax.fori_loop(0, place, one, state)


def node_tables():
    radical = math.sqrt(3.0 / 7.0)
    node_times = [0.0, (1.0 - radical) / 2.0, 0.5, (1.0 + radical) / 2.0, 1.0]
    integrals = np.zeros((4, 5))
    for column in range(5):
        coeffs = [1.0]
        for other_index in range(5):
            if other_index == column:
                continue
            other_time = node_times[other_index]
            scaling = node_times[column] - other_time
            grown = [0.0] * (len(coeffs) + 1)
            for exponent in range(len(coeffs)):
                grown[exponent + 1] += coeffs[exponent] / scaling
                grown[exponent] -= coeffs[exponent] * other_time / scaling
            coeffs = grown
        for section in range(4):
            integrals[section, column] = sum(
                (
                    coeffs[exponent]
                    * (
                        node_times[section + 1] ** (exponent + 1)
                        - node_times[section] ** (exponent + 1)
                    )
                    / (exponent + 1)
                    for exponent in range(len(coeffs))
                )
            )
    coarse = [0.0, 0.5, 1.0]
    interp = np.zeros((5, 3))
    for column in range(3):
        for section in range(5):
            weight = 1.0
            for other_index in range(3):
                if other_index != column:
                    weight = (
                        weight
                        * (node_times[section] - coarse[other_index])
                        / (coarse[column] - coarse[other_index])
                    )
            interp[section, column] = weight
    return (np.array(node_times), integrals, interp)


def stencil(padded):
    center = padded[..., 1:-1, :, :]
    widths = [(0, 0)] * (center.ndim - 2) + [(1, 1), (1, 1)]
    framed = jnp.pad(center, widths)
    return (
        padded[..., 2:, :, :]
        + padded[..., :-2, :, :]
        + framed[..., 2:, 1:-1]
        + framed[..., :-2, 1:-1]
        + framed[..., 1:-1, 2:]
        + framed[..., 1:-1, :-2]
        - 6.0 * center
    )


def laplace_one(field):
    return stencil(with_halo(field, (("space", 0),), 1))


def laplace_nodes(fields):
    return stencil(with_halo(fields, (("space", 1),), 1))


def sine_matrix(length, row_first, row_count, col_count):
    rows = jnp.arange(row_count, dtype=jnp.int32) + row_first + 1
    columns = jnp.arange(col_count, dtype=jnp.int32) + 1
    phase = rows[:, None] * columns[None, :] % (2 * (length + 1))
    return math.sqrt(2.0 / (length + 1)) * jnp.sin(
        math.pi / (length + 1) * phase.astype(jnp.float32)
    )


def eigen_weights(length, first, count):
    indices = (jnp.arange(count, dtype=jnp.int32) + first + 1).astype(jnp.float32)
    return 2.0 - 2.0 * jnp.cos(math.pi / (length + 1) * indices)


def compose(earlier, later):
    return (earlier[0] * later[0], later[0] * earlier[1] + later[1])


def body(initial, start_guess, forcing, step_size):
    depth, width_x, width_y = initial.shape
    length_z = depth * lax.axis_size("space")
    z_first = lax.axis_index("space") * depth
    position = lax.axis_index("tm")
    highest = lax.Precision.HIGHEST
    x_matrix = sine_matrix(width_x, 0, width_x, width_x)
    y_matrix = sine_matrix(width_y, 0, width_y, width_y)
    eigen = (
        eigen_weights(length_z, z_first, depth)[:, None, None]
        + eigen_weights(width_x, 0, width_x)[None, :, None]
        + eigen_weights(width_y, 0, width_y)[None, None, :]
    )

    def lateral(field):
        mixed = jnp.einsum("ai,zij->zaj", x_matrix, field, precision=highest)
        return jnp.einsum("zaj,bj->zab", mixed, y_matrix, precision=highest)

    def forward(field):
        flat = lateral(field).reshape(depth, width_x * width_y)
        shard_rows = lax.all_gather(flat, "space", axis=0, tiled=True)
        spectral = jnp.zeros_like(flat) + jnp.dot(
            sine_matrix(length_z, z_first, depth, shard_rows.shape[0]),
            shard_rows,
            precision=highest,
            preferred_element_type=jnp.float32,
        )
        return spectral.reshape(depth, width_x, width_y)

    node_times, integrals, interp = node_tables()
    full_step = step_size[0]
    half_step = 0.5 * full_step
    initial_hat = forward(initial)
    values = jnp.broadcast_to(start_guess[0][None], (5, depth, width_x, width_y))
    for sweep_round in range(ITERS):
        previous = shifted(values[4], "tm", 1)
        values = values.at[0].set(jnp.where(position == 0, initial, previous))
        lap_old = laplace_nodes(values)
        rates = lap_old + forcing[0]
        swept = [values[0]]
        lap_new = [lap_old[0]]
        for section in range(4):
            quadrature = sum(
                (float(integrals[section, column]) * rates[column] for column in range(5))
            )
            spacing = float(node_times[section + 1] - node_times[section])
            advanced = (
                swept[section]
                + full_step * spacing * (lap_new[section] - lap_old[section])
                + full_step * quadrature
            )
            swept.append(advanced)
            lap_new.append(laplace_one(advanced))
        new_rates = [lap_new[column] + forcing[0, column] for column in range(5)]
        first_half = full_step * sum(
            (
                float(integrals[0, column] + integrals[1, column]) * new_rates[column]
                for column in range(5)
            )
        )
        second_half = full_step * sum(
            (
                float(integrals[2, column] + integrals[3, column]) * new_rates[column]
                for column in range(5)
            )
        )
        left = first_half - half_step * lap_new[0]
        right = second_half - half_step * lap_new[2]
        forced = left + half_step * laplace_one(left) + right
        forced_hat = forward(forced)
        factor = 1.0 - half_step * eigen
        prefix_gain, prefix_sum = prefix(
            (factor * factor, forced_hat),
            "tm",
            compose,
            (jnp.ones_like(eigen), jnp.zeros_like(eigen)),
        )
        inverse_flat = (prefix_gain * initial_hat + prefix_sum).reshape(depth, width_x * width_y)
        accumulate_shard_rows = lax.all_gather(inverse_flat, "space", axis=0, tiled=True)
        physical = jnp.zeros_like(inverse_flat) + jnp.dot(
            sine_matrix(length_z, z_first, depth, accumulate_shard_rows.shape[0]),
            accumulate_shard_rows,
            precision=highest,
            preferred_element_type=jnp.float32,
        )
        coarse_first = lateral(physical.reshape(depth, width_x, width_y))
        coarse_middle = coarse_first + half_step * laplace_one(coarse_first) + left
        coarse_ending = coarse_middle + half_step * laplace_one(coarse_middle) + right
        deltas = [coarse_first - swept[0], coarse_middle - swept[2], coarse_ending - swept[4]]
        values = jnp.stack(
            [
                swept[section]
                + sum((float(interp[section, column]) * deltas[column] for column in range(3)))
                for section in range(5)
            ]
        )
    return values[None]


def solution(mesh):
    in_specs = (
        P("space", None, None),
        P("tm", "space", None, None),
        P("tm", None, "space", None, None),
        P("tm"),
    )
    out_specs = P("tm", None, "space", None, None)
    return jax.shard_map(body, mesh=mesh, in_specs=in_specs, out_specs=out_specs, check_vma=False)
```

profile of v0, /device:TPU:30, one launch (start us, length us, event | category | flops | bytes accessed | tf_op | source)
XLA Modules:
  0.0 293.3 jit_solution(4274129726435221056)
XLA Ops:
  8.5 5.3 %collective-permute-done = f32[2,128,128]{2,1,0:T(8,128)S(1)} collective-permute-done((f32[2,128,128]{2,1,0:T(8,128)}, f32[2,128,128]{2,1,0:T(8,128)S(1)}, u32[]{:S(2)}, u32[]{:S(2)}) %collective-permute-start) | collective-permute-done | bytes 131104 | tf_op jit(solution)/shard_map/ppermute | solution.py:28
  21.6 3.8 %collective-permute-done.2 = f32[5,1,128,128]{3,2,1,0:T(8,128)S(1)} collective-permute-done((f32[5,1,128,128]{3,2,1,0:T(8,128)S(1)}, f32[5,1,128,128]{3,2,1,0:T(8,128)S(1)}, u32[]{:S(2)}, u32[]{:S(2)}) %collective-permute-start.2) | collective-permute-done | bytes 327712 | tf_op jit(solution)/shard_map/ppermute | solution.py:17
  38.0 3.2 %collective-permute-done.6 = f32[1,128,128]{2,1,0:T(8,128)S(1)} collective-permute-done((f32[1,128,128]{2,1,0:T(8,128)S(1)}, f32[1,128,128]{2,1,0:T(8,128)S(1)}, u32[]{:S(2)}, u32[]{:S(2)}) %collective-permute-start.6) | collective-permute-done | bytes 65568 | tf_op jit(solution)/shard_map/ppermute | solution.py:17
  50.9 3.6 %collective-permute-start.9 = (f32[1,128,128]{2,1,0:T(8,128)S(1)}, f32[1,128,128]{2,1,0:T(8,128)S(1)}, u32[]{:S(2)}, u32[]{:S(2)}) collective-permute-start(f32[1,128,128]{2,1,0:T(8,128)S(1)} %get-tuple-element.187), channel_id=1, source_target_pairs={{1,0},{2,1},{3,2},{5,4},{6,5},{7,6},{9,8},{10,9},{11,10},{13,12},{... | collective-permute-start | bytes 196616 | tf_op jit(solution)/shard_map/ppermute | solution.py:20
  56.6 3.7 %collective-permute-start.11 = (f32[1,128,128]{2,1,0:T(8,128)S(1)}, f32[1,128,128]{2,1,0:T(8,128)S(1)}, u32[]{:S(2)}, u32[]{:S(2)}) collective-permute-start(f32[1,128,128]{2,1,0:T(8,128)S(1)} %get-tuple-element.185), channel_id=1, source_target_pairs={{1,0},{2,1},{3,2},{5,4},{6,5},{7,6},{9,8},{10,9},{11,10},{13,12},{... | collective-permute-start | bytes 196616 | tf_op jit(solution)/shard_map/ppermute | solution.py:20
  62.3 3.6 %collective-permute-done.12 = f32[1,128,128]{2,1,0:T(8,128)S(1)} collective-permute-done((f32[1,128,128]{2,1,0:T(8,128)S(1)}, f32[1,128,128]{2,1,0:T(8,128)S(1)}, u32[]{:S(2)}, u32[]{:S(2)}) %collective-permute-start.12) | collective-permute-done | bytes 65568 | tf_op jit(solution)/shard_map/ppermute | solution.py:17
  67.2 6.5 %all-gather = f32[4,2,16384]{2,1,0:T(2,128)S(1)} all-gather(f32[1,2,16384]{2,1,0:T(2,128)S(1)} %reshape.313), channel_id=1, replica_groups=mesh['tm'=8,'space'=4] {'space'}, dimensions={0}, use_global_device_ids=true | all-gather | bytes 655360 | tf_op jit(solution)/shard_map/all_gather | solution.py:149
  76.8 7.3 %all-gather.1 = f32[4,2,16384]{2,1,0:T(2,128)S(1)} all-gather(f32[1,2,16384]{2,1,0:T(2,128)S(1)} %reshape.315), channel_id=1, replica_groups=mesh['tm'=8,'space'=4] {'space'}, dimensions={0}, use_global_device_ids=true | all-gather | bytes 655360 | tf_op jit(solution)/shard_map/all_gather | solution.py:149
  85.2 29.8 %all-gather.11.cloned.1.call-done = f32[8,2,128,128]{3,2,1,0:T(8,128)} async-done(((f32[1,2,128,128]{3,2,1,0:T(8,128)}), f32[8,2,128,128]{3,2,1,0:T(8,128)}) %all-gather.11.cloned.1.call-update) | async-done | bytes 1048592 | tf_op jit(solution)/shard_map/all_gather | solution.py:33
  115.0 7.5 %while.26 = (s32[]{:T(128)}, f32[2,128,128]{2,1,0:T(8,128)S(1)}, f32[2,128,128]{2,1,0:T(8,128)S(1)}, s32[]{:T(128)}, f32[8,2,128,128]{3,2,1,0:T(8,128)}, /*index...) while((s32[]{:T(128)}, f32[2,128,128]{2,1,0:T(8,128)S(1)}, f32[2,128,128]{2,1,0:T(8,128)S(1)}, ...), condition=%wide.region_1.2_spmd, body=%wide.region_0.1_spmd.sunk | while | flops 98309 | bytes 786563 | solution.py:41
  122.6 6.5 %all-gather.2 = f32[4,2,16384]{2,1,0:T(2,128)S(1)} all-gather(f32[1,2,16384]{2,1,0:T(2,128)S(1)} %reshape.317), channel_id=1, replica_groups=mesh['tm'=8,'space'=4] {'space'}, dimensions={0}, use_global_device_ids=true | all-gather | bytes 655360 | tf_op jit(solution)/shard_map/all_gather | solution.py:207
  136.4 3.6 %collective-permute-done.14 = f32[1,128,128]{2,1,0:T(8,128)S(1)} collective-permute-done((f32[1,128,128]{2,1,0:T(8,128)S(1)}, f32[1,128,128]{2,1,0:T(8,128)S(1)}, u32[]{:S(2)}, u32[]{:S(2)}) %collective-permute-start.14) | collective-permute-done | bytes 65568 | tf_op jit(solution)/shard_map/ppermute | solution.py:17
  144.6 3.2 %collective-permute-done.16 = f32[1,128,128]{2,1,0:T(8,128)S(1)} collective-permute-done((f32[1,128,128]{2,1,0:T(8,128)S(1)}, f32[1,128,128]{2,1,0:T(8,128)S(1)}, u32[]{:S(2)}, u32[]{:S(2)}) %collective-permute-start.16) | collective-permute-done | bytes 65568 | tf_op jit(solution)/shard_map/ppermute | solution.py:17
  149.4 5.6 %collective-permute-done.17 = f32[2,128,128]{2,1,0:T(8,128)S(1)} collective-permute-done((f32[2,128,128]{2,1,0:T(8,128)S(1)}, f32[2,128,128]{2,1,0:T(8,128)S(1)}, u32[]{:S(2)}, u32[]{:S(2)}) %collective-permute-start.17) | collective-permute-done | bytes 131104 | tf_op jit(solution)/shard_map/ppermute | solution.py:28
  161.5 3.8 %collective-permute-done.19 = f32[5,1,128,128]{3,2,1,0:T(8,128)S(1)} collective-permute-done((f32[5,1,128,128]{3,2,1,0:T(8,128)S(1)}, f32[5,1,128,128]{3,2,1,0:T(8,128)S(1)}, u32[]{:S(2)}, u32[]{:S(2)}) %collective-permute-start.19) | collective-permute-done | bytes 327712 | tf_op jit(solution)/shard_map/ppermute | solution.py:17
  170.2 3.2 %collective-permute-done.21 = f32[1,128,128]{2,1,0:T(8,128)S(1)} collective-permute-done((f32[1,128,128]{2,1,0:T(8,128)S(1)}, f32[1,128,128]{2,1,0:T(8,128)S(1)}, u32[]{:S(2)}, u32[]{:S(2)}) %collective-permute-start.21) | collective-permute-done | bytes 65568 | tf_op jit(solution)/shard_map/ppermute | solution.py:17
  185.6 3.2 %collective-permute-done.25 = f32[1,128,128]{2,1,0:T(8,128)S(1)} collective-permute-done((f32[1,128,128]{2,1,0:T(8,128)S(1)}, f32[1,128,128]{2,1,0:T(8,128)S(1)}, u32[]{:S(2)}, u32[]{:S(2)}) %collective-permute-start.25) | collective-permute-done | bytes 65568 | tf_op jit(solution)/shard_map/ppermute | solution.py:17
  193.2 3.2 %collective-permute-done.27 = f32[1,128,128]{2,1,0:T(8,128)S(1)} collective-permute-done((f32[1,128,128]{2,1,0:T(8,128)S(1)}, f32[1,128,128]{2,1,0:T(8,128)S(1)}, u32[]{:S(2)}, u32[]{:S(2)}) %collective-permute-start.27) | collective-permute-done | bytes 65568 | tf_op jit(solution)/shard_map/ppermute | solution.py:17
  205.4 6.5 %all-gather.3 = f32[4,2,16384]{2,1,0:T(2,128)S(1)} all-gather(f32[1,2,16384]{2,1,0:T(2,128)S(1)} %reshape.319), channel_id=1, replica_groups=mesh['tm'=8,'space'=4] {'space'}, dimensions={0}, use_global_device_ids=true | all-gather | bytes 655360 | tf_op jit(solution)/shard_map/all_gather | solution.py:149
  213.7 39.1 %all-gather.13.cloned.1.call-done = f32[8,2,128,128]{3,2,1,0:T(8,128)} async-done(((f32[1,2,128,128]{3,2,1,0:T(8,128)}), f32[8,2,128,128]{3,2,1,0:T(8,128)}) %all-gather.13.cloned.1.call-update) | async-done | bytes 1048592 | tf_op jit(solution)/shard_map/all_gather | solution.py:33
  252.8 7.5 %while.27 = (s32[]{:T(128)}, f32[2,128,128]{2,1,0:T(8,128)S(1)}, f32[2,128,128]{2,1,0:T(8,128)S(1)}, s32[]{:T(128)}, f32[8,2,128,128]{3,2,1,0:T(8,128)}, /*index...) while((s32[]{:T(128)}, f32[2,128,128]{2,1,0:T(8,128)S(1)}, f32[2,128,128]{2,1,0:T(8,128)S(1)}, ...), condition=%wide.region_3.4_spmd, body=%wide.region_2.3_spmd.sunk | while | flops 98309 | bytes 786563 | solution.py:41
  260.5 6.5 %all-gather.4 = f32[4,2,16384]{2,1,0:T(2,128)S(1)} all-gather(f32[1,2,16384]{2,1,0:T(2,128)S(1)} %reshape.321), channel_id=1, replica_groups=mesh['tm'=8,'space'=4] {'space'}, dimensions={0}, use_global_device_ids=true | all-gather | bytes 655360 | tf_op jit(solution)/shard_map/all_gather | solution.py:207
  274.3 3.6 %collective-permute-done.31 = f32[1,128,128]{2,1,0:T(8,128)S(1)} collective-permute-done((f32[1,128,128]{2,1,0:T(8,128)S(1)}, f32[1,128,128]{2,1,0:T(8,128)S(1)}, u32[]{:S(2)}, u32[]{:S(2)}) %collective-permute-start.31) | collective-permute-done | bytes 65568 | tf_op jit(solution)/shard_map/ppermute | solution.py:17
  282.4 3.2 %collective-permute-done.33 = f32[1,128,128]{2,1,0:T(8,128)S(1)} collective-permute-done((f32[1,128,128]{2,1,0:T(8,128)S(1)}, f32[1,128,128]{2,1,0:T(8,128)S(1)}, u32[]{:S(2)}, u32[]{:S(2)}) %collective-permute-start.33) | collective-permute-done | bytes 65568 | tf_op jit(solution)/shard_map/ppermute | solution.py:17
  (165 shorter events, 120.2 us)
Async XLA Ops:
  6.5 78.6 %all-gather.9.cloned.1.call-start = ((), (), s32[]{:S(2)}) async-start(), calls=%async_computation | async-start | bytes 1179648 | tf_op jit(solution)/shard_map/all_gather | solution.py:33
  6.5 7.3 %collective-permute-start = (f32[2,128,128]{2,1,0:T(8,128)}, f32[2,128,128]{2,1,0:T(8,128)S(1)}, u32[]{:S(2)}, u32[]{:S(2)}) collective-permute-start(f32[2,128,128]{2,1,0:T(8,128)} %bitcast.276), channel_id=1, source_target_pairs={{0,4},{4,8},{8,12},{12,16},{16,20},{20,24},{24,28},{1,5},{5,9},{9,... | collective-permute-start | bytes 393224 | tf_op jit(solution)/shard_map/ppermute | solution.py:28
  14.9 6.6 %collective-permute-start.1 = (f32[5,1,128,128]{3,2,1,0:T(8,128)S(1)}, f32[5,1,128,128]{3,2,1,0:T(8,128)S(1)}, u32[]{:S(2)}, u32[]{:S(2)}) collective-permute-start(f32[5,1,128,128]{3,2,1,0:T(8,128)S(1)} %get-tuple-element.165), channel_id=1, source_target_pairs={{1,0},{2,1},{3,2},{5,4},{6,5},{7,6},{9,8},{10,9},{11,10},{13,12},{... | collective-permute-start | bytes 983048 | tf_op jit(solution)/shard_map/ppermute | solution.py:20
  17.0 8.4 %collective-permute-start.2 = (f32[5,1,128,128]{3,2,1,0:T(8,128)S(1)}, f32[5,1,128,128]{3,2,1,0:T(8,128)S(1)}, u32[]{:S(2)}, u32[]{:S(2)}) collective-permute-start(f32[5,1,128,128]{3,2,1,0:T(8,128)S(1)} %get-tuple-element.166), channel_id=1, source_target_pairs={{0,1},{1,2},{2,3},{4,5},{5,6},{6,7},{8,9},{9,10},{10,11},{12,13},{... | collective-permute-start | bytes 983048 | tf_op jit(solution)/shard_map/ppermute | solution.py:17
  27.8 5.6 %collective-permute-start.4 = (f32[1,128,128]{2,1,0:T(8,128)S(1)}, f32[1,128,128]{2,1,0:T(8,128)S(1)}, u32[]{:S(2)}, u32[]{:S(2)}) collective-permute-start(f32[1,128,128]{2,1,0:T(8,128)S(1)} %get-tuple-element.194), channel_id=1, source_target_pairs={{0,1},{1,2},{2,3},{4,5},{5,6},{6,7},{8,9},{9,10},{10,11},{12,13},{... | collective-permute-start | bytes 196616 | tf_op jit(solution)/shard_map/ppermute | solution.py:17
  31.0 83.9 %all-gather.11.cloned.1.call-start = ((), (), s32[]{:S(2)}) async-start(), calls=%async_computation.1 | async-start | bytes 1179648 | tf_op jit(solution)/shard_map/all_gather | solution.py:33
  35.5 5.6 %collective-permute-start.6 = (f32[1,128,128]{2,1,0:T(8,128)S(1)}, f32[1,128,128]{2,1,0:T(8,128)S(1)}, u32[]{:S(2)}, u32[]{:S(2)}) collective-permute-start(f32[1,128,128]{2,1,0:T(8,128)S(1)} %get-tuple-element.192), channel_id=1, source_target_pairs={{0,1},{1,2},{2,3},{4,5},{5,6},{6,7},{8,9},{9,10},{10,11},{12,13},{... | collective-permute-start | bytes 196616 | tf_op jit(solution)/shard_map/ppermute | solution.py:17
  43.2 5.6 %collective-permute-start.8 = (f32[1,128,128]{2,1,0:T(8,128)S(1)}, f32[1,128,128]{2,1,0:T(8,128)S(1)}, u32[]{:S(2)}, u32[]{:S(2)}) collective-permute-start(f32[1,128,128]{2,1,0:T(8,128)S(1)} %get-tuple-element.190), channel_id=1, source_target_pairs={{0,1},{1,2},{2,3},{4,5},{5,6},{6,7},{8,9},{9,10},{10,11},{12,13},{... | collective-permute-start | bytes 196616 | tf_op jit(solution)/shard_map/ppermute | solution.py:17
  49.0 5.6 %collective-permute-start.10 = (f32[1,128,128]{2,1,0:T(8,128)S(1)}, f32[1,128,128]{2,1,0:T(8,128)S(1)}, u32[]{:S(2)}, u32[]{:S(2)}) collective-permute-start(f32[1,128,128]{2,1,0:T(8,128)S(1)} %get-tuple-element.188), channel_id=1, source_target_pairs={{0,1},{1,2},{2,3},{4,5},{5,6},{6,7},{8,9},{9,10},{10,11},{12,13},{... | collective-permute-start | bytes 196616 | tf_op jit(solution)/shard_map/ppermute | solution.py:17
  56.6 5.7 %collective-permute-start.11 = (f32[1,128,128]{2,1,0:T(8,128)S(1)}, f32[1,128,128]{2,1,0:T(8,128)S(1)}, u32[]{:S(2)}, u32[]{:S(2)}) collective-permute-start(f32[1,128,128]{2,1,0:T(8,128)S(1)} %get-tuple-element.185), channel_id=1, source_target_pairs={{1,0},{2,1},{3,2},{5,4},{6,5},{7,6},{9,8},{10,9},{11,10},{13,12},{... | collective-permute-start | bytes 196616 | tf_op jit(solution)/shard_map/ppermute | solution.py:20
  60.3 5.6 %collective-permute-start.12 = (f32[1,128,128]{2,1,0:T(8,128)S(1)}, f32[1,128,128]{2,1,0:T(8,128)S(1)}, u32[]{:S(2)}, u32[]{:S(2)}) collective-permute-start(f32[1,128,128]{2,1,0:T(8,128)S(1)} %get-tuple-element.186), channel_id=1, source_target_pairs={{0,1},{1,2},{2,3},{4,5},{5,6},{6,7},{8,9},{9,10},{10,11},{12,13},{... | collective-permute-start | bytes 196616 | tf_op jit(solution)/shard_map/ppermute | solution.py:17
  75.5 177.3 %all-gather.13.cloned.1.call-start = ((), (), s32[]{:S(2)}) async-start(), calls=%async_computation.2 | async-start | bytes 1179648 | tf_op jit(solution)/shard_map/all_gather | solution.py:33
  134.5 5.6 %collective-permute-start.14 = (f32[1,128,128]{2,1,0:T(8,128)S(1)}, f32[1,128,128]{2,1,0:T(8,128)S(1)}, u32[]{:S(2)}, u32[]{:S(2)}) collective-permute-start(f32[1,128,128]{2,1,0:T(8,128)S(1)} %get-tuple-element.184), channel_id=1, source_target_pairs={{0,1},{1,2},{2,3},{4,5},{5,6},{6,7},{8,9},{9,10},{10,11},{12,13},{... | collective-permute-start | bytes 196616 | tf_op jit(solution)/shard_map/ppermute | solution.py:17
  142.1 5.6 %collective-permute-start.16 = (f32[1,128,128]{2,1,0:T(8,128)S(1)}, f32[1,128,128]{2,1,0:T(8,128)S(1)}, u32[]{:S(2)}, u32[]{:S(2)}) collective-permute-start(f32[1,128,128]{2,1,0:T(8,128)S(1)} %get-tuple-element.182), channel_id=1, source_target_pairs={{0,1},{1,2},{2,3},{4,5},{5,6},{6,7},{8,9},{9,10},{10,11},{12,13},{... | collective-permute-start | bytes 196616 | tf_op jit(solution)/shard_map/ppermute | solution.py:17
  148.1 6.9 %collective-permute-start.17 = (f32[2,128,128]{2,1,0:T(8,128)S(1)}, f32[2,128,128]{2,1,0:T(8,128)S(1)}, u32[]{:S(2)}, u32[]{:S(2)}) collective-permute-start(f32[2,128,128]{2,1,0:T(8,128)S(1)} %get-tuple-element.142), channel_id=1, source_target_pairs={{0,4},{4,8},{8,12},{12,16},{16,20},{20,24},{24,28},{1,5},{5,9},{9,... | collective-permute-start | bytes 393224 | tf_op jit(solution)/shard_map/ppermute | solution.py:28
  155.0 6.5 %collective-permute-start.18 = (f32[5,1,128,128]{3,2,1,0:T(8,128)S(1)}, f32[5,1,128,128]{3,2,1,0:T(8,128)S(1)}, u32[]{:S(2)}, u32[]{:S(2)}) collective-permute-start(f32[5,1,128,128]{3,2,1,0:T(8,128)S(1)} %get-tuple-element.163), channel_id=1, source_target_pairs={{1,0},{2,1},{3,2},{5,4},{6,5},{7,6},{9,8},{10,9},{11,10},{13,12},{... | collective-permute-start | bytes 983048 | tf_op jit(solution)/shard_map/ppermute | solution.py:20
  156.9 8.4 %collective-permute-start.19 = (f32[5,1,128,128]{3,2,1,0:T(8,128)S(1)}, f32[5,1,128,128]{3,2,1,0:T(8,128)S(1)}, u32[]{:S(2)}, u32[]{:S(2)}) collective-permute-start(f32[5,1,128,128]{3,2,1,0:T(8,128)S(1)} %get-tuple-element.164), channel_id=1, source_target_pairs={{0,1},{1,2},{2,3},{4,5},{5,6},{6,7},{8,9},{9,10},{10,11},{12,13},{... | collective-permute-start | bytes 983048 | tf_op jit(solution)/shard_map/ppermute | solution.py:17
  167.8 5.6 %collective-permute-start.21 = (f32[1,128,128]{2,1,0:T(8,128)S(1)}, f32[1,128,128]{2,1,0:T(8,128)S(1)}, u32[]{:S(2)}, u32[]{:S(2)}) collective-permute-start(f32[1,128,128]{2,1,0:T(8,128)S(1)} %get-tuple-element.180), channel_id=1, source_target_pairs={{0,1},{1,2},{2,3},{4,5},{5,6},{6,7},{8,9},{9,10},{10,11},{12,13},{... | collective-permute-start | bytes 196616 | tf_op jit(solution)/shard_map/ppermute | solution.py:17
  175.5 5.6 %collective-permute-start.23 = (f32[1,128,128]{2,1,0:T(8,128)S(1)}, f32[1,128,128]{2,1,0:T(8,128)S(1)}, u32[]{:S(2)}, u32[]{:S(2)}) collective-permute-start(f32[1,128,128]{2,1,0:T(8,128)S(1)} %get-tuple-element.178), channel_id=1, source_target_pairs={{0,1},{1,2},{2,3},{4,5},{5,6},{6,7},{8,9},{9,10},{10,11},{12,13},{... | collective-permute-start | bytes 196616 | tf_op jit(solution)/shard_map/ppermute | solution.py:17
  183.1 5.6 %collective-permute-start.25 = (f32[1,128,128]{2,1,0:T(8,128)S(1)}, f32[1,128,128]{2,1,0:T(8,128)S(1)}, u32[]{:S(2)}, u32[]{:S(2)}) collective-permute-start(f32[1,128,128]{2,1,0:T(8,128)S(1)} %get-tuple-element.176), channel_id=1, source_target_pairs={{0,1},{1,2},{2,3},{4,5},{5,6},{6,7},{8,9},{9,10},{10,11},{12,13},{... | collective-permute-start | bytes 196616 | tf_op jit(solution)/shard_map/ppermute | solution.py:17
  190.8 5.6 %collective-permute-start.27 = (f32[1,128,128]{2,1,0:T(8,128)S(1)}, f32[1,128,128]{2,1,0:T(8,128)S(1)}, u32[]{:S(2)}, u32[]{:S(2)}) collective-permute-start(f32[1,128,128]{2,1,0:T(8,128)S(1)} %get-tuple-element.174), channel_id=1, source_target_pairs={{0,1},{1,2},{2,3},{4,5},{5,6},{6,7},{8,9},{9,10},{10,11},{12,13},{... | collective-permute-start | bytes 196616 | tf_op jit(solution)/shard_map/ppermute | solution.py:17
  198.5 5.6 %collective-permute-start.29 = (f32[1,128,128]{2,1,0:T(8,128)S(1)}, f32[1,128,128]{2,1,0:T(8,128)S(1)}, u32[]{:S(2)}, u32[]{:S(2)}) collective-permute-start(f32[1,128,128]{2,1,0:T(8,128)S(1)} %get-tuple-element.172), channel_id=1, source_target_pairs={{0,1},{1,2},{2,3},{4,5},{5,6},{6,7},{8,9},{9,10},{10,11},{12,13},{... | collective-permute-start | bytes 196616 | tf_op jit(solution)/shard_map/ppermute | solution.py:17
  272.3 5.6 %collective-permute-start.31 = (f32[1,128,128]{2,1,0:T(8,128)S(1)}, f32[1,128,128]{2,1,0:T(8,128)S(1)}, u32[]{:S(2)}, u32[]{:S(2)}) collective-permute-start(f32[1,128,128]{2,1,0:T(8,128)S(1)} %get-tuple-element.170), channel_id=1, source_target_pairs={{0,1},{1,2},{2,3},{4,5},{5,6},{6,7},{8,9},{9,10},{10,11},{12,13},{... | collective-permute-start | bytes 196616 | tf_op jit(solution)/shard_map/ppermute | solution.py:17
  280.0 5.6 %collective-permute-start.33 = (f32[1,128,128]{2,1,0:T(8,128)S(1)}, f32[1,128,128]{2,1,0:T(8,128)S(1)}, u32[]{:S(2)}, u32[]{:S(2)}) collective-permute-start(f32[1,128,128]{2,1,0:T(8,128)S(1)} %get-tuple-element.168), channel_id=1, source_target_pairs={{0,1},{1,2},{2,3},{4,5},{5,6},{6,7},{8,9},{9,10},{10,11},{12,13},{... | collective-permute-start | bytes 196616 | tf_op jit(solution)/shard_map/ppermute | solution.py:17
  (16 other events, 73.3 us)
Sparse Core Ops, SparseCore 0:
  31.2 38.9 all-gather.8
  75.6 39.3 all-gather.10
  213.8 38.9 all-gather.12
where the time goes:
time: 295 us; the launch traced here: 293 us
  waiting for transfers between devices  135 us (46%)
  starting transfers between devices  76.1 us (26%)
  blocking collectives  33.3 us (11%)
  other arithmetic  18.9 us (6%)
  between operations  14.8 us (5%)
  matrix products  9.32 us (3%)
  local copies, waits for them, and re-layouts  5.59 us (2%)
    all_gather x3, waiting for transfers between devices, prefix(): gathered = jax.tree.map(lambda a: lax.all_gather(a, axis), part)  68.9 us
    ppermute x16, waiting for transfers between devices, with_halo(): lax.ppermute(lax.slice_in_dim(block, block.shape[dim] - width, None, axis...  49 us
    ppermute x16, starting transfers between devices, with_halo(): lax.ppermute(lax.slice_in_dim(block, block.shape[dim] - width, None, axis...  36.8 us
    ppermute x16, starting transfers between devices, with_halo(): lax.ppermute(lax.slice_in_dim(block, 0, width, axis=dim), axis, backward)  36.6 us
    all_gather x3, blocking collectives, forward(): shard_rows = lax.all_gather(flat, 'space', axis=0, tiled=True)  20.3 us
    add x14, other arithmetic, compose(): return (earlier[0] * later[0], later[0] * earlier[1] + later[1])  14.7 us
    all_gather x2, blocking collectives, body(): lax.all_gather(inverse_flat, 'space', axis=0, tiled=True)  13 us
    ppermute x2, waiting for transfers between devices, shifted(): lax.ppermute(value, axis, [(source, source + steps) for source in range(f...  10.9 us
  transfers between devices with their start and end apart: 37, of which 22 were waited for; matrix products, arithmetic and copies ran while one was open for 2% of the time, Pallas kernels for 0%

commit v1 on v0

v1 whole, which is shorter than its diff:
```python
import functools
import math

import jax
import jax.numpy as jnp
import numpy as np
from jax import lax
from jax.experimental import pallas as pl
from jax.experimental.pallas import tpu as pltpu
from jax.sharding import Mesh
from jax.sharding import PartitionSpec as P

TILE = 8


def node_tables():
    radical = math.sqrt(3.0 / 7.0)
    node_times = [0.0, (1.0 - radical) / 2.0, 0.5, (1.0 + radical) / 2.0, 1.0]
    integrals = np.zeros((4, 5))
    for column in range(5):
        coeffs = [1.0]
        for other_index in range(5):
            if other_index == column:
                continue
            other_time = node_times[other_index]
            scaling = node_times[column] - other_time
            grown = [0.0] * (len(coeffs) + 1)
            for exponent in range(len(coeffs)):
                grown[exponent + 1] += coeffs[exponent] / scaling
                grown[exponent] -= coeffs[exponent] * other_time / scaling
            coeffs = grown
        for section in range(4):
            integrals[section, column] = sum(
                coeffs[exponent]
                * (node_times[section + 1] ** (exponent + 1) - node_times[section] ** (exponent + 1))
                / (exponent + 1)
                for exponent in range(len(coeffs))
            )
    coarse = [0.0, 0.5, 1.0]
    interp = np.zeros((5, 3))
    for column in range(3):
        for section in range(5):
            weight = 1.0
            for other_index in range(3):
                if other_index != column:
                    weight = (
                        weight
                        * (node_times[section] - coarse[other_index])
                        / (coarse[column] - coarse[other_index])
                    )
            interp[section, column] = weight
    return (np.array(node_times), integrals, interp)


TIMES, QUAD, INTERP = node_tables()
SPACING = np.diff(TIMES)
LEFT = QUAD[0] + QUAD[1]
RIGHT = QUAD[2] + QUAD[3]


def sine(length):
    index = np.arange(1, length + 1)
    return math.sqrt(2.0 / (length + 1)) * np.sin(math.pi / (length + 1) * np.outer(index, index))


def eigen(length):
    return 2.0 - 2.0 * np.cos(math.pi / (length + 1) * np.arange(1, length + 1))


def halves(matrix):
    high = matrix.astype(jnp.bfloat16).astype(np.float64)
    return high, matrix - high


def right_table(length):
    high, low = halves(sine(length))
    return np.block([[high, low], [high, np.zeros_like(high)]]).astype(jnp.bfloat16)


def left_table(length):
    high, low = halves(sine(length))
    return np.block([[high, high], [low, np.zeros_like(high)]]).astype(jnp.bfloat16)


def split(value):
    high = value.astype(jnp.bfloat16)
    return high, (value - high.astype(jnp.float32)).astype(jnp.bfloat16)


def times_sine(value, table):
    width = value.shape[-1]
    both = jnp.dot(
        jnp.concatenate(split(value), axis=1), table, preferred_element_type=jnp.float32
    )
    return both[:, :width] + both[:, width:]


def sine_times(value, table):
    width = value.shape[0]
    both = jnp.dot(
        table, jnp.concatenate(split(value), axis=0), preferred_element_type=jnp.float32
    )
    return both[:width] + both[width:]


def sine_list(values):
    count = len(values)
    matrix = sine(count)
    half = count // 2
    even = [values[i] + values[count - 1 - i] for i in range(half)]
    odd = [values[i] - values[count - 1 - i] for i in range(half)]
    middle = [values[half]] if count % 2 else []
    result = []
    for k in range(count):
        terms = even + middle if k % 2 == 0 else odd
        result.append(sum(float(matrix[k, i]) * term for i, term in enumerate(terms)))
    return result


def combine(weights, values):
    return sum(float(w) * v for w, v in zip(weights, values) if w != 0.0)


def sweep(first, nodes, forced, scaled):
    swept = [first]
    for m in range(4):
        inner = combine(QUAD[m], nodes)
        if m:
            inner = inner + float(SPACING[m]) * (swept[m] - nodes[m])
        swept.append(swept[m] + (scaled * inner + forced[m]))
    left = scaled * (combine(LEFT, swept) - 0.5 * swept[0]) + (forced[0] + forced[1])
    right = scaled * (combine(RIGHT, swept) - 0.5 * swept[2]) + (forced[2] + forced[3])
    return swept, left, right


def chain(start, left, right, gain):
    middle = gain * start + left
    return middle, gain * middle + right


def correct(swept, start, middle, ending):
    deltas = [start - swept[0], middle - swept[2], ending - swept[4]]
    return [
        start,
        swept[1] + combine(INTERP[1], deltas),
        middle,
        swept[3] + combine(INTERP[3], deltas),
        ending,
    ]


def march(guesses, forced, scaled, state, final):
    before, first, second = state
    fields = []
    for j, guess in enumerate(guesses):
        gain = 1.0 + 0.5 * scaled[j]
        swept, left, right = sweep(before, [before] + [guess] * 4, forced[j], scaled[j])
        middle, ending = chain(first, left, right, gain)
        nodes = correct(swept, first, middle, ending)
        swept, left, right = sweep(first, nodes, forced[j], scaled[j])
        middle, last = chain(second, left, right, gain)
        if final:
            fields.append(correct(swept, second, middle, last))
        before, first, second = guess, ending, last
    return fields if final else (before, first, second)


def forward_kernel(dims, step_ref, init_ref, guess_ref, forcing_ref, right_ref, left_ref, out_ref):
    depth, groups, per, lo, pieces = dims
    step = step_ref[0]
    width = init_ref.shape[1]
    planes = []
    for d in range(depth):
        planes.append(init_ref[d])
        planes.append(guess_ref[0, d])
        samples = [forcing_ref[0, j, d] for j in range(5)]
        for m in range(4):
            planes.append(step * combine(QUAD[m], samples))
    mixed = times_sine(jnp.concatenate(planes, axis=0), right_ref[...])
    mixed = [mixed[i * width : (i + 1) * width] for i in range(len(planes))]
    spectral = []
    for i in range(0, len(mixed), 2):
        pair = sine_times(jnp.concatenate(mixed[i : i + 2], axis=1), left_ref[...])
        spectral += [pair[:, : pair.shape[1] // 2], pair[:, pair.shape[1] // 2 :]]
    fields = 5
    per_plane = len(planes) // depth
    for d in range(depth):
        for f in range(fields):
            row = (f * depth + d) * per
            out_ref[:, row : row + per, :] = spectral[d * per_plane + 1 + f].reshape(
                groups, per, -1
            )
    mine = lax.axis_index("lo")
    rows = per // pieces
    share = None
    for i in range(lo):
        tile = spectral[(i // pieces) * per_plane].reshape(groups, per, -1)
        offset = (i % pieces) * rows
        tile = tile[:, offset : offset + rows]
        share = tile if share is None else jnp.where(mine == i, tile, share)
    base = fields * depth * per
    out_ref[:, base : base + rows, :] = share
    out_ref[:, base + rows :, :] = jnp.full(
        (groups, out_ref.shape[1] - base - rows, out_ref.shape[2]), step, jnp.float32
    )


def owner_weights(dims, space, x_ref, y_ref):
    depth, groups, per, lo, pieces = dims
    owner = lax.axis_index("lo") * space + lax.axis_index("space")
    return x_ref[pl.ds(owner * per, per), :] + y_ref[...]


def gather_kernel(dims, space, got_ref, x_ref, y_ref, modes_ref, start_ref, state_ref):
    depth, groups, per, lo, pieces = dims
    count = depth * space
    base = 5 * depth * per
    rows = per // pieces
    for j in range(lo):
        for f in range(5):
            tiles = []
            for z in range(count):
                row = (f * depth + z % depth) * per
                tiles.append(got_ref[j * space + z // depth, row : row + per, :])
            for z, tile in enumerate(sine_list(tiles)):
                modes_ref[j, f, z] = tile
    tiles = []
    for z in range(count):
        first = (z % depth) * pieces
        tiles.append(
            jnp.concatenate(
                [
                    got_ref[i * space + z // depth, base : base + rows, :]
                    for i in range(first, first + pieces)
                ],
                axis=0,
            )
        )
    for z, tile in enumerate(sine_list(tiles)):
        start_ref[z] = tile
    for j in range(lo):
        state_ref[3, j] = jnp.broadcast_to(
            got_ref[j * space, base + rows : base + rows + 1, :], state_ref.shape[2:]
        )
    advance(dims, space, modes_ref, state_ref, x_ref, y_ref, lambda z: (start_ref[z],) * 3)


def advance(dims, space, modes_ref, state_ref, x_ref, y_ref, state_of):
    depth, groups, per, lo, pieces = dims
    count = depth * space
    plane = owner_weights(dims, space, x_ref, y_ref)
    steps = [state_ref[3, j] for j in range(lo)]
    weights = eigen(count)
    for z in range(count):
        neg = -(plane + float(weights[z]))
        guesses = [modes_ref[j, 0, z] for j in range(lo)]
        forced = [[modes_ref[j, 1 + m, z] for m in range(4)] for j in range(lo)]
        scaled = [steps[j] * neg for j in range(lo)]
        for i, tile in enumerate(march(guesses, forced, scaled, state_of(z), False)):
            state_ref[i, z] = tile


def middle_kernel(dims, space, modes_ref, start_ref, own_ref, came_ref, x_ref, y_ref, state_ref):
    lo = dims[3]
    head = lax.axis_index("hi") == 0
    for j in range(lo):
        state_ref[3, j] = own_ref[3, j]
    advance(
        dims,
        space,
        modes_ref,
        state_ref,
        x_ref,
        y_ref,
        lambda z: tuple(jnp.where(head, start_ref[z], came_ref[i, z]) for i in range(3)),
    )


def finish_kernel(dims, space, modes_ref, start_ref, own_ref, came_ref, x_ref, y_ref, out_ref, tmp_ref):
    depth, groups, per, lo, pieces = dims
    count = depth * space
    head = lax.axis_index("hi") == 0
    plane = owner_weights(dims, space, x_ref, y_ref)
    steps = [own_ref[3, j] for j in range(lo)]
    weights = eigen(count)
    for z in range(count):
        neg = -(plane + float(weights[z]))
        guesses = [modes_ref[j, 0, z] for j in range(lo)]
        forced = [[modes_ref[j, 1 + m, z] for m in range(4)] for j in range(lo)]
        scaled = [steps[j] * neg for j in range(lo)]
        start = start_ref[z]
        state = tuple(jnp.where(head, start, came_ref[i, z]) for i in range(3))
        for j, nodes in enumerate(march(guesses, forced, scaled, state, True)):
            for m in range(5):
                tmp_ref[j, m, z] = nodes[m]
    for j in range(lo):
        for m in range(5):
            tiles = sine_list([tmp_ref[j, m, z] for z in range(count)])
            for z in range(count):
                row = (m * depth + z % depth) * per
                out_ref[j * space + z // depth, row : row + per, :] = tiles[z]


def backward_kernel(dims, got_ref, right_ref, left_ref, out_ref):
    depth, groups, per, lo, pieces = dims
    rows, width = got_ref.shape[1:]
    mixed = times_sine(got_ref[...].reshape(groups * rows, width), right_ref[...])
    mixed = mixed.reshape(groups, rows, width)
    planes = [
        mixed[:, i * per : (i + 1) * per, :].reshape(groups * per, width)
        for i in range(5 * depth)
    ]
    for i in range(0, len(planes), 2):
        pair = sine_times(jnp.concatenate(planes[i : i + 2], axis=1), left_ref[...])
        out_ref[0, i // depth, i % depth] = pair[:, :width]
        out_ref[0, (i + 1) // depth, (i + 1) % depth] = pair[:, width:]


VMEM = pl.BlockSpec(memory_space=pltpu.VMEM)
SMEM = pl.BlockSpec(memory_space=pltpu.SMEM)


def call(kernel, shapes, count, scalars=0, scratch=()):
    many = isinstance(shapes, (list, tuple)) and isinstance(shapes[0], tuple)
    outs = [jax.ShapeDtypeStruct(s, jnp.float32) for s in (shapes if many else [shapes])]
    return pl.pallas_call(
        kernel,
        out_shape=outs if many else outs[0],
        in_specs=[SMEM] * scalars + [VMEM] * (count - scalars),
        out_specs=[VMEM] * len(outs) if many else VMEM,
        scratch_shapes=list(scratch),
    )


def body(initial, start_guess, forcing, step_size):
    depth, width_x, width_y = initial.shape
    space, lo, hi = (lax.axis_size(a) for a in ("space", "lo", "hi"))
    groups = space * lo
    per = width_x // groups
    pieces = lo // depth
    dims = (depth, groups, per, lo, pieces)
    count = depth * space
    right = jnp.asarray(right_table(width_y))
    left = jnp.asarray(left_table(width_x))
    x_weights = jnp.asarray(
        np.broadcast_to(eigen(width_x)[:, None], (width_x, width_y)).astype(np.float32)
    )
    y_weights = jnp.asarray(eigen(width_y)[None, :].astype(np.float32))

    rows = 5 * depth * per
    send = call(
        functools.partial(forward_kernel, dims), (groups, rows + TILE, width_y), 6, 1
    )(step_size, initial, start_guess, forcing, right, left)
    got = lax.all_to_all(send, ("lo", "space"), 0, 0, tiled=True)
    modes, start, state = call(
        functools.partial(gather_kernel, dims, space),
        [
            (lo, 5, count, per, width_y),
            (count, per, width_y),
            (4, max(count, lo), per, width_y),
        ],
        3,
    )(got, x_weights, y_weights)
    onward = [(i, i + 1) for i in range(hi - 1)]
    came = lax.ppermute(state[:3], "hi", onward)
    for _ in range(hi - 2):
        state = call(
            functools.partial(middle_kernel, dims, space), (4, max(count, lo), per, width_y), 6
        )(modes, start, state, came, x_weights, y_weights)
        came = lax.ppermute(state[:3], "hi", onward)
    send = call(
        functools.partial(finish_kernel, dims, space),
        (groups, rows, width_y),
        6,
        scratch=[pltpu.VMEM((lo, 5, count, per, width_y), jnp.float32)],
    )(modes, start, state, came, x_weights, y_weights)
    got = lax.all_to_all(send, ("lo", "space"), 0, 0, tiled=True)
    return call(
        functools.partial(backward_kernel, dims), (1, 5, depth, width_x, width_y), 3
    )(got, right, left)


def solution(mesh):
    steps, space = mesh.devices.shape
    time = ("hi", "lo")
    specs = (
        P("space", None, None),
        P(time, "space", None, None),
        P(time, None, "space", None, None),
        P(time),
    )

    def run(initial, start_guess, forcing, step_size):
        width = initial.shape[1]
        lo = max(
            d for d in range(1, steps + 1) if steps % d == 0 and width % (TILE * d * space) == 0
        )
        whole = Mesh(mesh.devices.reshape(steps // lo, lo, space), ("hi", "lo", "space"))
        return jax.shard_map(
            body,
            mesh=whole,
            in_specs=specs,
            out_specs=P(time, None, "space", None, None),
            check_vma=False,
        )(initial, start_guess, forcing, step_size)

    return run
```

time: 295 us -> 56.3 us (0.19)
  the two profiles are of different devices: /device:TPU:30 before, /device:TPU:0 now
where the time goes in v1:
time: 56.3 us; the launch traced here: 55.9 us
  blocking collectives  35.2 us (63%)
  Pallas kernels  11.8 us (21%)
  starting transfers between devices  4.49 us (8%)
  waiting for transfers between devices  2.19 us (4%)
  local copies, waits for them, and re-layouts  1.54 us (3%)
  between operations  0.66 us (1%)
    all_to_all x2, blocking collectives, body(): got = lax.all_to_all(send, ('lo', 'space'), 0, 0, tiled=True)  35.2 us
    ppermute x1, starting transfers between devices, body(): came = lax.ppermute(state[:3], 'hi', onward)  4.49 us
    pallas_call x1, Pallas kernels, body(): call(functools.partial(finish_kernel, dims, space), (groups, rows, width_...  3.08 us
    pallas_call x1, Pallas kernels, body(): call(functools.partial(backward_kernel, dims), (1, 5, depth, width_x, wid...  2.95 us
    pallas_call x1, Pallas kernels, body(): call(functools.partial(forward_kernel, dims), (groups, rows + TILE, width...  2.95 us
    pallas_call x1, Pallas kernels, body(): call(functools.partial(gather_kernel, dims, space), [(lo, 5, count, per,...  2.78 us
    ppermute x1, waiting for transfers between devices, body(): came = lax.ppermute(state[:3], 'hi', onward)  2.19 us
  transfers between devices with their start and end apart: 1, of which 1 were waited for; matrix products, arithmetic and copies ran while one was open for 0% of the time, Pallas kernels for 0%

profile of v1, /device:TPU:0, one launch (start us, length us, event | category | flops | bytes accessed | tf_op | source)
XLA Modules:
  0.0 55.9 jit_solution(4314229296921159896)
XLA Ops:
  0.7 3.0 %shard_map.82 = f32[16,88,128]{2,1,0:T(8,128)} custom-call(f32[1]{0:T(128)S(6)} %copy.9.step_ref, f32[2,128,128]{2,1,0:T(8,128)} %init_ref.1, f32[1,2,128,128]{3,2,1,0:T(8,128)} %guess_ref.1, f32[1,5,2,128,128]{4,3,2,1,0:T(8,128)} %forcing_ref.1, bf16[256,256]{1,0:T(8,128)(2,1)} %constant.8.clone.right_ref, bf16[256,256]{1,0:T(8,128)(2,1)} %constant.9.clone.left_ref), custom_call_target="tpu_custom_call" | custom-call | tf_op jit(solution)/shard_map/pallas_call | solution.py:351
  3.6 19.0 %all_to_all.10.got_ref = f32[16,88,128]{2,1,0:T(8,128)} all-to-all(f32[16,88,128]{2,1,0:T(8,128)} %shard_map.82), channel_id=1, replica_groups=mesh['hi'=2,'lo'=4,'space'=4] {'lo','space'}, dimensions={0} | all-to-all | bytes 1441792 | tf_op jit(solution)/shard_map/all_to_all | solution.py:354
  22.6 2.8 %shard_map.83 = (f32[4,5,8,8,128]{4,3,2,1,0:T(8,128)}, f32[8,8,128]{2,1,0:T(8,128)}, f32[4,8,8,128]{3,2,1,0:T(8,128)}) custom-call(f32[16,88,128]{2,1,0:T(8,128)} %all_to_all.10.got_ref, f32[128,128]{1,0:T(8,128)} %constant.10.clone.x_ref, f32[1,128]{1,0:T(1,128)} %constant.11.clone.y_ref), custom_call_target="tpu_custom_call" | custom-call | tf_op jit(solution)/shard_map/pallas_call | solution.py:355
  25.4 0.9 %slice.3 = f32[3,8,8,128]{3,2,1,0:T(8,128)S(1)} slice(f32[4,8,8,128]{3,2,1,0:T(8,128)} %get-tuple-element.10.own_ref), slice={[0:3], [0:8], [0:8], [0:128]} | slice | bytes 196608 | tf_op jit(solution)/shard_map/slice | solution.py:365
  26.3 4.5 %collective-permute-start = (f32[3,8,8,128]{3,2,1,0:T(8,128)S(1)}, f32[3,8,8,128]{3,2,1,0:T(8,128)S(1)}, u32[]{:S(2)}, u32[]{:S(2)}) collective-permute-start(f32[3,8,8,128]{3,2,1,0:T(8,128)S(1)} %slice.3), channel_id=1, source_target_pairs={{0,16},{1,17},{2,18},{3,19},{4,20},{5,21},{6,22},{7,23},{8,24},{9,... | collective-permute-start | bytes 294920 | tf_op jit(solution)/shard_map/ppermute | solution.py:365
  30.8 2.2 %collective-permute-done.came_ref = f32[3,8,8,128]{3,2,1,0:T(8,128)S(1)} collective-permute-done((f32[3,8,8,128]{3,2,1,0:T(8,128)S(1)}, f32[3,8,8,128]{3,2,1,0:T(8,128)S(1)}, u32[]{:S(2)}, u32[]{:S(2)}) %collective-permute-start) | collective-permute-done | bytes 98336 | tf_op jit(solution)/shard_map/ppermute | solution.py:365
  33.0 0.0 copy-start
  33.0 0.6 %copy-done = f32[3,8,8,128]{3,2,1,0:T(8,128)} copy-done((f32[3,8,8,128]{3,2,1,0:T(8,128)}, f32[3,8,8,128]{3,2,1,0:T(8,128)S(1)}, u32[]{:S(2)}) %copy-start) | copy-done | bytes 98328
  33.6 3.1 %shard_map.84 = f32[16,80,128]{2,1,0:T(8,128)} custom-call(f32[4,5,8,8,128]{4,3,2,1,0:T(8,128)} %get-tuple-element.8.modes_ref, f32[8,8,128]{2,1,0:T(8,128)} %get-tuple-element.9.start_ref, f32[4,8,8,128]{3,2,1,0:T(8,128)} %get-tuple-element.10.own_ref, f32[3,8,8,128]{3,2,1,0:T(8,128)} %copy-done, f32[128,128]{1,0:T(8,128)} %constant.10.clone.x_ref, ...), custom_call_target="tpu_custom_call" | custom-call | tf_op jit(solution)/shard_map/pallas_call | solution.py:371
  36.7 16.2 %all_to_all.11.got_ref = f32[16,80,128]{2,1,0:T(8,128)} all-to-all(f32[16,80,128]{2,1,0:T(8,128)} %shard_map.84), channel_id=1, replica_groups=mesh['hi'=2,'lo'=4,'space'=4] {'lo','space'}, dimensions={0} | all-to-all | bytes 1310720 | tf_op jit(solution)/shard_map/all_to_all | solution.py:377
  52.9 3.0 %shard_map.85 = f32[1,5,2,128,128]{4,3,2,1,0:T(8,128)} custom-call(f32[16,80,128]{2,1,0:T(8,128)} %all_to_all.11.got_ref, bf16[256,256]{1,0:T(8,128)(2,1)} %constant.8.clone.right_ref, bf16[256,256]{1,0:T(8,128)(2,1)} %constant.9.clone.left_ref), custom_call_target="tpu_custom_call" | custom-call | tf_op jit(solution)/shard_map/pallas_call | solution.py:378
Async XLA Ops:
  26.3 6.7 %collective-permute-start = (f32[3,8,8,128]{3,2,1,0:T(8,128)S(1)}, f32[3,8,8,128]{3,2,1,0:T(8,128)S(1)}, u32[]{:S(2)}, u32[]{:S(2)}) collective-permute-start(f32[3,8,8,128]{3,2,1,0:T(8,128)S(1)} %slice.3), channel_id=1, source_target_pairs={{0,16},{1,17},{2,18},{3,19},{4,20},{5,21},{6,22},{7,23},{8,24},{9,... | collective-permute-start | bytes 294920 | tf_op jit(solution)/shard_map/ppermute | solution.py:365
  33.0 0.6 %copy-start = (f32[3,8,8,128]{3,2,1,0:T(8,128)}, f32[3,8,8,128]{3,2,1,0:T(8,128)S(1)}, u32[]{:S(2)}) copy-start(f32[3,8,8,128]{3,2,1,0:T(8,128)S(1)} %collective-permute-done.came_ref) | copy-start | bytes 294916

commit v2 on v1

v2 whole, which is shorter than its diff:
```python
import functools
import math

import jax
import jax.numpy as jnp
import numpy as np
from jax import lax
from jax.experimental import pallas as pl
from jax.experimental.pallas import tpu as pltpu
from jax.sharding import Mesh
from jax.sharding import PartitionSpec as P

TILE = 8


def node_tables():
    radical = math.sqrt(3.0 / 7.0)
    node_times = [0.0, (1.0 - radical) / 2.0, 0.5, (1.0 + radical) / 2.0, 1.0]
    integrals = np.zeros((4, 5))
    for column in range(5):
        coeffs = [1.0]
        for other_index in range(5):
            if other_index == column:
                continue
            other_time = node_times[other_index]
            scaling = node_times[column] - other_time
            grown = [0.0] * (len(coeffs) + 1)
            for exponent in range(len(coeffs)):
                grown[exponent + 1] += coeffs[exponent] / scaling
                grown[exponent] -= coeffs[exponent] * other_time / scaling
            coeffs = grown
        for section in range(4):
            integrals[section, column] = sum(
                coeffs[exponent]
                * (node_times[section + 1] ** (exponent + 1) - node_times[section] ** (exponent + 1))
                / (exponent + 1)
                for exponent in range(len(coeffs))
            )
    coarse = [0.0, 0.5, 1.0]
    interp = np.zeros((5, 3))
    for column in range(3):
        for section in range(5):
            weight = 1.0
            for other_index in range(3):
                if other_index != column:
                    weight = (
                        weight
                        * (node_times[section] - coarse[other_index])
                        / (coarse[column] - coarse[other_index])
                    )
            interp[section, column] = weight
    return (np.array(node_times), integrals, interp)


TIMES, QUAD, INTERP = node_tables()
SPACING = np.diff(TIMES)
LEFT = QUAD[0] + QUAD[1]
RIGHT = QUAD[2] + QUAD[3]


def sine(length):
    index = np.arange(1, length + 1)
    return math.sqrt(2.0 / (length + 1)) * np.sin(math.pi / (length + 1) * np.outer(index, index))


def eigen(length):
    return 2.0 - 2.0 * np.cos(math.pi / (length + 1) * np.arange(1, length + 1))


def halves(matrix):
    high = matrix.astype(jnp.bfloat16).astype(np.float64)
    return high, matrix - high


def right_table(length):
    high, low = halves(sine(length))
    return np.block([[high, low], [high, np.zeros_like(high)]]).astype(jnp.bfloat16)


def left_table(length):
    high, low = halves(sine(length))
    return np.block([[high, high], [low, np.zeros_like(high)]]).astype(jnp.bfloat16)


def split(value):
    high = value.astype(jnp.bfloat16)
    return high, (value - high.astype(jnp.float32)).astype(jnp.bfloat16)


def times_sine(value, table):
    width = value.shape[-1]
    both = jnp.dot(
        jnp.concatenate(split(value), axis=1), table, preferred_element_type=jnp.float32
    )
    return both[:, :width] + both[:, width:]


def sine_times(value, table):
    width = value.shape[0]
    both = jnp.dot(
        table, jnp.concatenate(split(value), axis=0), preferred_element_type=jnp.float32
    )
    return both[:width] + both[width:]


def sine_list(values):
    count = len(values)
    matrix = sine(count)
    half = count // 2
    even = [values[i] + values[count - 1 - i] for i in range(half)]
    odd = [values[i] - values[count - 1 - i] for i in range(half)]
    middle = [values[half]] if count % 2 else []
    result = []
    for k in range(count):
        terms = even + middle if k % 2 == 0 else odd
        result.append(sum(float(matrix[k, i]) * term for i, term in enumerate(terms)))
    return result


def combine(weights, values):
    return sum(float(w) * v for w, v in zip(weights, values) if w != 0.0)


def sweep(first, nodes, forced, scaled):
    swept = [first]
    for m in range(4):
        inner = combine(QUAD[m], nodes)
        if m:
            inner = inner + float(SPACING[m]) * (swept[m] - nodes[m])
        swept.append(swept[m] + (scaled * inner + forced[m]))
    left = scaled * (combine(LEFT, swept) - 0.5 * swept[0]) + (forced[0] + forced[1])
    right = scaled * (combine(RIGHT, swept) - 0.5 * swept[2]) + (forced[2] + forced[3])
    return swept, left, right


def chain(start, left, right, gain):
    middle = gain * start + left
    return middle, gain * middle + right


def correct(swept, start, middle, ending):
    deltas = [start - swept[0], middle - swept[2], ending - swept[4]]
    return [
        start,
        swept[1] + combine(INTERP[1], deltas),
        middle,
        swept[3] + combine(INTERP[3], deltas),
        ending,
    ]


def march(guesses, forced, scaled, state, final):
    before, first, second = state
    fields = []
    for j, guess in enumerate(guesses):
        gain = 1.0 + 0.5 * scaled[j]
        swept, left, right = sweep(before, [before] + [guess] * 4, forced[j], scaled[j])
        middle, ending = chain(first, left, right, gain)
        nodes = correct(swept, first, middle, ending)
        swept, left, right = sweep(first, nodes, forced[j], scaled[j])
        middle, last = chain(second, left, right, gain)
        if final:
            fields.append(correct(swept, second, middle, last))
        before, first, second = guess, ending, last
    return fields if final else (before, first, second)


def forward_kernel(
    dims, step_ref, init_hbm, guess_hbm, forcing_hbm, right_hbm, left_hbm, out_ref,
    init_ref, guess_ref, forcing_ref, right_ref, left_ref, sems, table_sems,
):
    depth, groups, per, lo, pieces = dims
    tables = [
        pltpu.make_async_copy(right_hbm, right_ref, table_sems.at[0]),
        pltpu.make_async_copy(left_hbm, left_ref, table_sems.at[1]),
    ]
    copies = []
    for d in range(depth):
        copies.append(
            [
                pltpu.make_async_copy(init_hbm.at[d], init_ref.at[d], sems.at[d, 0]),
                pltpu.make_async_copy(guess_hbm.at[0, d], guess_ref.at[d], sems.at[d, 1]),
                pltpu.make_async_copy(forcing_hbm.at[0, :, d], forcing_ref.at[d], sems.at[d, 2]),
            ]
        )
        for copy in copies[d] + (tables if d == 0 else []):
            copy.start()
    step = step_ref[0]
    width = init_ref.shape[1]
    starts = []
    for d in range(depth):
        for copy in copies[d]:
            copy.wait()
        samples = [forcing_ref[d, j] for j in range(5)]
        planes = [init_ref[d], guess_ref[d]]
        planes += [step * combine(QUAD[m], samples) for m in range(4)]
        if d == 0:
            tables[0].wait()
        mixed = times_sine(jnp.concatenate(planes, axis=0), right_ref[...])
        for i in range(0, len(planes), 2):
            pair = jnp.concatenate(
                [mixed[k * width : (k + 1) * width] for k in (i, i + 1)], axis=1
            )
            if d == 0 and i == 0:
                tables[1].wait()
            pair = sine_times(pair, left_ref[...])
            half = pair.shape[1] // 2
            for f, plane in ((i - 1, pair[:, :half]), (i, pair[:, half:])):
                tiles = plane.reshape(groups, per, half)
                if f < 0:
                    starts.append(tiles)
                else:
                    row = (f * depth + d) * per
                    out_ref[:, row : row + per, :] = tiles
    mine = lax.axis_index("lo")
    rows = per // pieces
    share = None
    for i in range(lo):
        offset = (i % pieces) * rows
        tile = starts[i // pieces][:, offset : offset + rows]
        share = tile if share is None else jnp.where(mine == i, tile, share)
    base = 5 * depth * per
    out_ref[:, base : base + rows, :] = share
    out_ref[:, base + rows :, :] = jnp.full(
        (groups, out_ref.shape[1] - base - rows, out_ref.shape[2]), step, jnp.float32
    )


def to_modes(dims, space, got_ref, modes_ref, steps_ref):
    depth, groups, per, lo, pieces = dims
    base = 5 * depth * per + per // pieces
    for j in range(lo):
        for f in range(5):
            tiles = []
            for z in range(depth * space):
                row = (f * depth + z % depth) * per
                tiles.append(got_ref[j * space + z // depth, row : row + per, :])
            for z, tile in enumerate(sine_list(tiles)):
                modes_ref[j, f, z] = tile
        steps_ref[j] = jnp.broadcast_to(
            got_ref[j * space, base : base + 1, :], steps_ref.shape[1:]
        )


def initial_modes(dims, space, got_ref):
    depth, groups, per, lo, pieces = dims
    base = 5 * depth * per
    rows = per // pieces
    tiles = []
    for z in range(depth * space):
        first = (z % depth) * pieces
        parts = [
            got_ref[i * space + z // depth, base : base + rows, :]
            for i in range(first, first + pieces)
        ]
        tiles.append(jnp.concatenate(parts, axis=0))
    return sine_list(tiles)


def per_mode(dims, space, modes_ref, steps_ref, x_ref, y_ref, state_of, final):
    depth, groups, per, lo, pieces = dims
    owner = lax.axis_index("lo") * space + lax.axis_index("space")
    plane = x_ref[pl.ds(owner * per, per), :] + y_ref[...]
    steps = [steps_ref[j] for j in range(lo)]
    for z, weight in enumerate(eigen(depth * space)):
        neg = -(plane + float(weight))
        guesses = [modes_ref[j, 0, z] for j in range(lo)]
        forced = [[modes_ref[j, 1 + m, z] for m in range(4)] for j in range(lo)]
        yield z, march(guesses, forced, [s * neg for s in steps], state_of(z), final)


def first_kernel(dims, space, got_ref, x_ref, y_ref, state_ref, modes_ref, steps_ref, start_ref):
    @pl.when(lax.axis_index("hi") == 0)
    def _():
        to_modes(dims, space, got_ref, modes_ref, steps_ref)
        for z, tile in enumerate(initial_modes(dims, space, got_ref)):
            start_ref[z] = tile
        ends = per_mode(
            dims, space, modes_ref, steps_ref, x_ref, y_ref, lambda z: (start_ref[z],) * 3, False
        )
        for z, state in ends:
            for i in range(3):
                state_ref[i, z] = state[i]


def write_fields(dims, space, results, tmp_ref, out_ref):
    depth, groups, per, lo, pieces = dims
    for z, slices in results:
        for j, nodes in enumerate(slices):
            for m in range(5):
                tmp_ref[j, m, z] = nodes[m]
    for j in range(lo):
        for m in range(5):
            tiles = sine_list([tmp_ref[j, m, z] for z in range(depth * space)])
            for z, tile in enumerate(tiles):
                row = (m * depth + z % depth) * per
                out_ref[j * space + z // depth, row : row + per, :] = tile


def window_kernel(
    dims, space, got_ref, modes_in, steps_in, start_ref, x_ref, y_ref,
    modes_ref, steps_ref, out_ref, tmp_ref,
):
    head = lax.axis_index("hi") == 0

    @pl.when(head)
    def _():
        results = per_mode(
            dims, space, modes_ref, steps_ref, x_ref, y_ref, lambda z: (start_ref[z],) * 3, True
        )
        write_fields(dims, space, results, tmp_ref, out_ref)

    @pl.when(jnp.logical_not(head))
    def _():
        to_modes(dims, space, got_ref, modes_ref, steps_ref)


def middle_kernel(dims, space, state_in, modes_ref, steps_ref, came_ref, x_ref, y_ref, state_ref):
    @pl.when(lax.axis_index("hi") > 0)
    def _():
        ends = per_mode(
            dims, space, modes_ref, steps_ref, x_ref, y_ref,
            lambda z: tuple(came_ref[i, z] for i in range(3)), False,
        )
        for z, state in ends:
            for i in range(3):
                state_ref[i, z] = state[i]


def finish_kernel(
    dims, space, out_in, modes_ref, steps_ref, came_ref, x_ref, y_ref, out_ref, tmp_ref
):
    @pl.when(lax.axis_index("hi") > 0)
    def _():
        results = per_mode(
            dims, space, modes_ref, steps_ref, x_ref, y_ref,
            lambda z: tuple(came_ref[i, z] for i in range(3)), True,
        )
        write_fields(dims, space, results, tmp_ref, out_ref)


def backward_kernel(dims, got_ref, right_ref, left_ref, out_hbm, out_ref, sems):
    depth, groups, per, lo, pieces = dims
    rows, width = got_ref.shape[1:]
    copies = []
    for i in range(0, 5 * depth, 2):
        mixed = times_sine(
            got_ref[:, i * per : (i + 2) * per, :].reshape(groups * 2 * per, width), right_ref[...]
        ).reshape(groups, 2 * per, width)
        pair = jnp.concatenate(
            [
                mixed[:, :per].reshape(groups * per, width),
                mixed[:, per:].reshape(groups * per, width),
            ],
            axis=1,
        )
        pair = sine_times(pair, left_ref[...])
        for k, plane in ((i, pair[:, :width]), (i + 1, pair[:, width:])):
            out_ref[k] = plane
            copy = pltpu.make_async_copy(
                out_ref.at[k], out_hbm.at[0, k // depth, k % depth], sems.at[k]
            )
            copy.start()
            copies.append(copy)
    for copy in copies:
        copy.wait()


VMEM = pl.BlockSpec(memory_space=pltpu.VMEM)
SMEM = pl.BlockSpec(memory_space=pltpu.SMEM)
HBM = pl.BlockSpec(memory_space=pltpu.HBM)


def call(kernel, shapes, in_specs, scratch=(), out_spec=VMEM, aliases=None):
    return pl.pallas_call(
        kernel,
        out_shape=[jax.ShapeDtypeStruct(s, jnp.float32) for s in shapes],
        in_specs=in_specs,
        out_specs=[out_spec] * len(shapes),
        scratch_shapes=list(scratch),
        input_output_aliases=aliases or {},
        compiler_params=pltpu.CompilerParams(vmem_limit_bytes=12 * 2**20),
    )


def body(initial, start_guess, forcing, step_size):
    depth, width_x, width_y = initial.shape
    space, lo, hi = (lax.axis_size(a) for a in ("space", "lo", "hi"))
    groups = space * lo
    per = width_x // groups
    pieces = lo // depth
    dims = (depth, groups, per, lo, pieces)
    count = depth * space
    right = jnp.asarray(right_table(width_y))
    left = jnp.asarray(left_table(width_x))
    x_weights = jnp.asarray(
        np.broadcast_to(eigen(width_x)[:, None], (width_x, width_y)).astype(np.float32)
    )
    y_weights = jnp.asarray(eigen(width_y)[None, :].astype(np.float32))
    tile = (per, width_y)
    bind = functools.partial
    plane = (width_x, width_y)

    rows = 5 * depth * per
    (send,) = call(
        bind(forward_kernel, dims),
        [(groups, rows + TILE, width_y)],
        [SMEM] + [HBM] * 5,
        [
            pltpu.VMEM((depth, *plane), jnp.float32),
            pltpu.VMEM((depth, *plane), jnp.float32),
            pltpu.VMEM((depth, 5, *plane), jnp.float32),
            pltpu.VMEM(right.shape, right.dtype),
            pltpu.VMEM(left.shape, left.dtype),
            pltpu.SemaphoreType.DMA((depth, 3)),
            pltpu.SemaphoreType.DMA((2,)),
        ],
    )(step_size, initial, start_guess, forcing, right, left)
    got = lax.all_to_all(send, ("lo", "space"), 0, 0, tiled=True)
    state_shape, modes_shape, steps_shape = (3, count, *tile), (lo, 5, count, *tile), (lo, *tile)
    state, modes, steps, start = call(
        bind(first_kernel, dims, space),
        [state_shape, modes_shape, steps_shape, (count, *tile)],
        [VMEM] * 3,
    )(got, x_weights, y_weights)
    onward = [(i, i + 1) for i in range(hi - 1)]
    came = lax.ppermute(state, "hi", onward)
    field_scratch = [pltpu.VMEM((lo, 5, count, *tile), jnp.float32)]
    modes, steps, send = call(
        bind(window_kernel, dims, space),
        [modes_shape, steps_shape, (groups, rows, width_y)],
        [VMEM] * 6,
        field_scratch,
        aliases={1: 0, 2: 1},
    )(got, modes, steps, start, x_weights, y_weights)
    for _ in range(hi - 2):
        (state,) = call(
            bind(middle_kernel, dims, space), [state_shape], [VMEM] * 6, aliases={0: 0}
        )(state, modes, steps, came, x_weights, y_weights)
        came = lax.ppermute(state, "hi", onward)
    (send,) = call(
        bind(finish_kernel, dims, space),
        [(groups, rows, width_y)],
        [VMEM] * 6,
        field_scratch,
        aliases={0: 0},
    )(send, modes, steps, came, x_weights, y_weights)
    got = lax.all_to_all(send, ("lo", "space"), 0, 0, tiled=True)
    (fields,) = call(
        bind(backward_kernel, dims),
        [(1, 5, depth, width_x, width_y)],
        [VMEM] * 3,
        [
            pltpu.VMEM((5 * depth, *plane), jnp.float32),
            pltpu.SemaphoreType.DMA((5 * depth,)),
        ],
        HBM,
    )(got, right, left)
    return fields


def solution(mesh):
    steps, space = mesh.devices.shape
    time = ("hi", "lo")
    specs = (
        P("space", None, None),
        P(time, "space", None, None),
        P(time, None, "space", None, None),
        P(time),
    )

    def run(initial, start_guess, forcing, step_size):
        width = initial.shape[1]
        lo = max(
            d for d in range(1, steps + 1) if steps % d == 0 and width % (TILE * d * space) == 0
        )
        whole = Mesh(mesh.devices.reshape(steps // lo, lo, space), ("hi", "lo", "space"))
        return jax.shard_map(
            body,
            mesh=whole,
            in_specs=specs,
            out_specs=P(time, None, "space", None, None),
            check_vma=False,
        )(initial, start_guess, forcing, step_size)

    return run
```

time: 56.3 us -> 51.3 us (0.911)
  Pallas kernels: 11.8 us -> 5.62 us
  local copies, waits for them, and re-layouts: 1.54 us -> 4.71 us
  waiting for transfers between devices: 2.19 us -> 1.1 us
  starting transfers between devices: 4.49 us -> 3.51 us
    pallas_call x4 -> x5, Pallas kernels: 11.8 us -> 5.62 us  [the longest x1 2.13 us: body(): call(bind(forward_kernel, dims), [(groups, rows + TILE, width_y)], [SMEM]...]
    unnamed x2 -> x16, local copies, waits for them, and re-layouts: 0.64 us -> 4.71 us
    ppermute x1, waiting for transfers between devices: 2.19 us -> 1.1 us  [body(): came = lax.ppermute(state, 'hi', onward)]
    ppermute x1, starting transfers between devices: 4.49 us -> 3.51 us  [body(): came = lax.ppermute(state, 'hi', onward)]
    slice x1 -> x0, local copies, waits for them, and re-layouts: 0.9 us -> none  [body(): came = lax.ppermute(state[:3], 'hi', onward)]
  transfers between devices with their start and end apart: 1 -> 1, of which waited for: 1 -> 1; matrix products, arithmetic and copies ran while one was open for 0% -> 0% of each run, Pallas kernels for 0% -> 2%
where the time goes in v2:
time: 51.3 us; the launch traced here: 50.5 us
  blocking collectives  34.9 us (68%)
  Pallas kernels  5.62 us (11%)
  local copies, waits for them, and re-layouts  4.71 us (9%)
  starting transfers between devices  3.51 us (7%)
  waiting for transfers between devices  1.1 us (2%)
  between operations  0.71 us (1%)
    all_to_all x2, blocking collectives, body(): got = lax.all_to_all(send, ('lo', 'space'), 0, 0, tiled=True)  34.9 us
    unnamed x16, local copies, waits for them, and re-layouts  4.71 us
    ppermute x1, starting transfers between devices, body(): came = lax.ppermute(state, 'hi', onward)  3.51 us
    pallas_call x1, Pallas kernels, body(): call(bind(forward_kernel, dims), [(groups, rows + TILE, width_y)], [SMEM]...  2.13 us
    pallas_call x1, Pallas kernels, body(): call(bind(backward_kernel, dims), [(1, 5, depth, width_x, width_y)], [VME...  1.43 us
    ppermute x1, waiting for transfers between devices, body(): came = lax.ppermute(state, 'hi', onward)  1.1 us
    pallas_call x1, Pallas kernels, body(): call(bind(window_kernel, dims, space), [modes_shape, steps_shape, (groups...  1.08 us
  transfers between devices with their start and end apart: 1, of which 1 were waited for; matrix products, arithmetic and copies ran while one was open for 0% of the time, Pallas kernels for 2%

profile of v2, /device:TPU:0, one launch (start us, length us, event | category | flops | bytes accessed | tf_op | source)
XLA Modules:
  0.0 50.5 jit_solution(4268382771938696427)
XLA Ops:
  0.7 0.0 copy-start
  0.7 1.1 %copy-done = f32[1,5,2,128,128]{4,3,2,1,0:T(8,128)S(1)} copy-done((f32[1,5,2,128,128]{4,3,2,1,0:T(8,128)S(1)}, f32[1,5,2,128,128]{4,3,2,1,0:T(8,128)}, u32[]{:S(2)}) %copy-start) | copy-done | bytes 655384
  1.7 0.0 copy-start.2
  1.7 0.9 %copy-done.2 = bf16[256,256]{1,0:T(8,128)(2,1)S(1)} copy-done((bf16[256,256]{1,0:T(8,128)(2,1)S(1)}, bf16[256,256]{1,0:T(8,128)(2,1)}, u32[]{:S(2)}) %copy-start.2) | copy-done | bytes 131096
  2.6 0.0 copy-start.3
  2.6 0.9 %copy-done.3 = bf16[256,256]{1,0:T(8,128)(2,1)S(1)} copy-done((bf16[256,256]{1,0:T(8,128)(2,1)S(1)}, bf16[256,256]{1,0:T(8,128)(2,1)}, u32[]{:S(2)}) %copy-start.3) | copy-done | bytes 131096
  3.5 0.0 copy-start.5
  3.6 0.9 %copy-done.5 = f32[2,128,128]{2,1,0:T(8,128)S(1)} copy-done((f32[2,128,128]{2,1,0:T(8,128)S(1)}, f32[2,128,128]{2,1,0:T(8,128)}, u32[]{:S(2)}) %copy-start.5) | copy-done | bytes 131096
  4.5 0.0 copy-start.6
  4.5 0.9 %copy-done.6 = f32[1,2,128,128]{3,2,1,0:T(8,128)S(1)} copy-done((f32[1,2,128,128]{3,2,1,0:T(8,128)S(1)}, f32[1,2,128,128]{3,2,1,0:T(8,128)}, u32[]{:S(2)}) %copy-start.6) | copy-done | bytes 131096
  5.4 2.1 %shard_map.82 = f32[16,88,128]{2,1,0:T(8,128)S(1)} custom-call(f32[1]{0:T(128)S(6)} %copy.15.step_ref, f32[2,128,128]{2,1,0:T(8,128)S(1)} %copy-done.5, f32[1,2,128,128]{3,2,1,0:T(8,128)S(1)} %copy-done.6, f32[1,5,2,128,128]{4,3,2,1,0:T(8,128)S(1)} %copy-done, bf16[256,256]{1,0:T(8,128)(2,1)S(1)} %copy-done.3, bf16[256,256]{1,0:T(8,128)(2,1)S(1)} %copy-done.2), custom_call_target="tpu_custom_call" | custom-call | tf_op jit(solution)/shard_map/pallas_call | solution.py:405
  7.5 0.0 copy-start.1
  7.5 0.0 copy-start.7
  7.5 18.9 %all_to_all.10.got_ref = f32[16,88,128]{2,1,0:T(8,128)S(1)} all-to-all(f32[16,88,128]{2,1,0:T(8,128)S(1)} %shard_map.82), channel_id=1, replica_groups=mesh['hi'=2,'lo'=4,'space'=4] {'lo','space'}, dimensions={0} | all-to-all | bytes 1441792 | tf_op jit(solution)/shard_map/all_to_all | solution.py:419
  26.4 0.0 copy-done.1
  26.4 0.0 copy-done.7
  26.4 1.0 %shard_map.83 = (f32[3,8,8,128]{3,2,1,0:T(8,128)S(1)}, f32[4,5,8,8,128]{4,3,2,1,0:T(8,128)S(1)}, f32[4,8,128]{2,1,0:T(8,128)S(1)}, f32[8,8,128]{2,1,0:T(8,128)S(1)}) custom-call(f32[16,88,128]{2,1,0:T(8,128)S(1)} %all_to_all.10.got_ref, f32[128,128]{1,0:T(8,128)S(1)} %copy-done.1, f32[1,128]{1,0:T(1,128)S(1)} %copy-done.7), custom_call_target="tpu_custom_call" | custom-call | tf_op jit(solution)/shard_map/pallas_call | solution.py:421
  27.4 3.5 %collective-permute-start = (f32[3,8,8,128]{3,2,1,0:T(8,128)S(1)}, f32[3,8,8,128]{3,2,1,0:T(8,128)S(1)}, u32[]{:S(2)}, u32[]{:S(2)}) collective-permute-start(f32[3,8,8,128]{3,2,1,0:T(8,128)S(1)} %get-tuple-element.18), channel_id=1, source_target_pairs={{0,16},{1,17},{2,18},{3,19},{4,20},{5,21},{6,22},{7,23},{8,24},{9,... | collective-permute-start | bytes 294920 | tf_op jit(solution)/shard_map/ppermute | solution.py:427
  30.9 1.1 %shard_map.84 = (f32[4,5,8,8,128]{4,3,2,1,0:T(8,128)S(1)}, f32[4,8,128]{2,1,0:T(8,128)S(1)}, f32[16,80,128]{2,1,0:T(8,128)S(1)}) custom-call(f32[16,88,128]{2,1,0:T(8,128)S(1)} %all_to_all.10.got_ref, f32[4,5,8,8,128]{4,3,2,1,0:T(8,128)S(1)} %get-tuple-element.12.modes_in, ...), custom_call_target="tpu_custom_call", output_to_operand_aliasing={{0}: (1, {}), {1}: (2, {})} | custom-call | tf_op jit(solution)/shard_map/pallas_call | solution.py:429
  32.0 1.1 %collective-permute-done.came_ref = f32[3,8,8,128]{3,2,1,0:T(8,128)S(1)} collective-permute-done((f32[3,8,8,128]{3,2,1,0:T(8,128)S(1)}, f32[3,8,8,128]{3,2,1,0:T(8,128)S(1)}, u32[]{:S(2)}, u32[]{:S(2)}) %collective-permute-start) | collective-permute-done | bytes 98336 | tf_op jit(solution)/shard_map/ppermute | solution.py:427
  33.1 0.0 copy-start.4
  33.1 16.0 %all_to_all.11.got_ref = f32[16,80,128]{2,1,0:T(8,128)S(1)} all-to-all(f32[16,80,128]{2,1,0:T(8,128)S(1)} %shard_map.85), channel_id=1, replica_groups=mesh['hi'=2,'lo'=4,'space'=4] {'lo','space'}, dimensions={0} | all-to-all | bytes 1310720 | tf_op jit(solution)/shard_map/all_to_all | solution.py:448
  49.1 0.0 copy-done.4
  49.1 1.4 %shard_map.86 = f32[1,5,2,128,128]{4,3,2,1,0:T(8,128)} custom-call(f32[16,80,128]{2,1,0:T(8,128)S(1)} %all_to_all.11.got_ref, bf16[256,256]{1,0:T(8,128)(2,1)S(1)} %copy-done.4, bf16[256,256]{1,0:T(8,128)(2,1)S(1)} %copy-done.2), custom_call_target="tpu_custom_call" | custom-call | tf_op jit(solution)/shard_map/pallas_call | solution.py:449
  (1 shorter events, 0.0 us)
Async XLA Ops:
  0.7 1.1 %copy-start = (f32[1,5,2,128,128]{4,3,2,1,0:T(8,128)S(1)}, f32[1,5,2,128,128]{4,3,2,1,0:T(8,128)}, u32[]{:S(2)}) copy-start(f32[1,5,2,128,128]{4,3,2,1,0:T(8,128)} %forcing_hbm.1) | copy-start | bytes 1966084
  1.7 0.9 %copy-start.2 = (bf16[256,256]{1,0:T(8,128)(2,1)S(1)}, bf16[256,256]{1,0:T(8,128)(2,1)}, u32[]{:S(2)}) copy-start(bf16[256,256]{1,0:T(8,128)(2,1)} %constant.9.clone.left_hbm.left_ref) | copy-start | bytes 393220
  2.6 0.9 %copy-start.3 = (bf16[256,256]{1,0:T(8,128)(2,1)S(1)}, bf16[256,256]{1,0:T(8,128)(2,1)}, u32[]{:S(2)}) copy-start(bf16[256,256]{1,0:T(8,128)(2,1)} %constant.8.clone.right_hbm.right_ref) | copy-start | bytes 393220
  3.5 0.9 %copy-start.5 = (f32[2,128,128]{2,1,0:T(8,128)S(1)}, f32[2,128,128]{2,1,0:T(8,128)}, u32[]{:S(2)}) copy-start(f32[2,128,128]{2,1,0:T(8,128)} %init_hbm.1) | copy-start | bytes 393220
  4.5 0.9 %copy-start.6 = (f32[1,2,128,128]{3,2,1,0:T(8,128)S(1)}, f32[1,2,128,128]{3,2,1,0:T(8,128)}, u32[]{:S(2)}) copy-start(f32[1,2,128,128]{3,2,1,0:T(8,128)} %guess_hbm.1) | copy-start | bytes 393220
  7.5 18.9 %copy-start.1 = (f32[128,128]{1,0:T(8,128)S(1)}, f32[128,128]{1,0:T(8,128)}, u32[]{:S(2)}) copy-start(f32[128,128]{1,0:T(8,128)} %constant.10.clone.x_ref) | copy-start | bytes 196612
  7.5 18.9 %copy-start.7 = (f32[1,128]{1,0:T(1,128)S(1)}, f32[1,128]{1,0:T(1,128)}, u32[]{:S(2)}) copy-start(f32[1,128]{1,0:T(1,128)} %constant.11.clone.y_ref) | copy-start | bytes 1540
  27.4 5.7 %collective-permute-start = (f32[3,8,8,128]{3,2,1,0:T(8,128)S(1)}, f32[3,8,8,128]{3,2,1,0:T(8,128)S(1)}, u32[]{:S(2)}, u32[]{:S(2)}) collective-permute-start(f32[3,8,8,128]{3,2,1,0:T(8,128)S(1)} %get-tuple-element.18), channel_id=1, source_target_pairs={{0,16},{1,17},{2,18},{3,19},{4,20},{5,21},{6,22},{7,23},{8,24},{9,... | collective-permute-start | bytes 294920 | tf_op jit(solution)/shard_map/ppermute | solution.py:427
  33.1 16.0 %copy-start.4 = (bf16[256,256]{1,0:T(8,128)(2,1)S(1)}, bf16[256,256]{1,0:T(8,128)(2,1)}, u32[]{:S(2)}) copy-start(bf16[256,256]{1,0:T(8,128)(2,1)} %constant.8.clone.right_hbm.right_ref) | copy-start | bytes 393220

commit v3 on v2

--- a/solution.py
+++ b/solution.py
@@ -371,6 +371,10 @@
 HBM = pl.BlockSpec(memory_space=pltpu.HBM)
 
 
+def in_hbm(value):
+    return pltpu.with_memory_space_constraint(value, pltpu.HBM)
+
+
 def call(kernel, shapes, in_specs, scratch=(), out_spec=VMEM, aliases=None):
     return pl.pallas_call(
         kernel,
@@ -415,7 +419,7 @@
             pltpu.SemaphoreType.DMA((depth, 3)),
             pltpu.SemaphoreType.DMA((2,)),
         ],
-    )(step_size, initial, start_guess, forcing, right, left)
+    )(step_size, *(in_hbm(a) for a in (initial, start_guess, forcing, right, left)))
     got = lax.all_to_all(send, ("lo", "space"), 0, 0, tiled=True)
     state_shape, modes_shape, steps_shape = (3, count, *tile), (lo, 5, count, *tile), (lo, *tile)
     state, modes, steps, start = call(

time: 51.3 us -> 46.9 us (0.914)
  local copies, waits for them, and re-layouts: 4.71 us -> 0.02 us
    unnamed x16 -> x8, local copies, waits for them, and re-layouts: 4.71 us -> 0.02 us
where the time goes in v3:
time: 46.9 us; the launch traced here: 46.2 us
  blocking collectives  34.9 us (74%)
  Pallas kernels  5.99 us (13%)
  starting transfers between devices  3.51 us (7%)
  waiting for transfers between devices  1.1 us (2%)
  between operations  0.7 us (1%)
    all_to_all x2, blocking collectives, body(): got = lax.all_to_all(send, ('lo', 'space'), 0, 0, tiled=True)  34.9 us
    ppermute x1, starting transfers between devices, body(): came = lax.ppermute(state, 'hi', onward)  3.51 us
    pallas_call x1, Pallas kernels, body(): call(bind(forward_kernel, dims), [(groups, rows + TILE, width_y)], [SMEM]...  2.5 us
    pallas_call x1, Pallas kernels, body(): call(bind(backward_kernel, dims), [(1, 5, depth, width_x, width_y)], [VME...  1.43 us
    ppermute x1, waiting for transfers between devices, body(): came = lax.ppermute(state, 'hi', onward)  1.1 us
    pallas_call x1, Pallas kernels, body(): call(bind(window_kernel, dims, space), [modes_shape, steps_shape, (groups...  1.08 us
    pallas_call x1, Pallas kernels, body(): call(bind(first_kernel, dims, space), [state_shape, modes_shape, steps_sh...  0.98 us
  transfers between devices with their start and end apart: 1, of which 1 were waited for; matrix products, arithmetic and copies ran while one was open for 0% of the time, Pallas kernels for 2%

profile of v3, /device:TPU:0, one launch (start us, length us, event | category | flops | bytes accessed | tf_op | source)
XLA Modules:
  0.0 46.2 jit_solution(1295187846419340925)
XLA Ops:
  0.7 2.5 %shard_map.82 = f32[16,88,128]{2,1,0:T(8,128)S(1)} custom-call(f32[1]{0:T(128)S(6)} %copy.15.step_ref, f32[2,128,128]{2,1,0:T(8,128)} %init_hbm.1, f32[1,2,128,128]{3,2,1,0:T(8,128)} %guess_hbm.1, f32[1,5,2,128,128]{4,3,2,1,0:T(8,128)} %forcing_hbm.1, bf16[256,256]{1,0:T(8,128)(2,1)} %constant.8.clone.right_hbm.right_ref, ...), custom_call_target="tpu_custom_call" | custom-call | tf_op jit(solution)/shard_map/pallas_call | solution.py:409
  3.2 0.0 copy-start
  3.2 0.0 copy-start.3
  3.2 18.9 %all_to_all.10.got_ref = f32[16,88,128]{2,1,0:T(8,128)S(1)} all-to-all(f32[16,88,128]{2,1,0:T(8,128)S(1)} %shard_map.82), channel_id=1, replica_groups=mesh['hi'=2,'lo'=4,'space'=4] {'lo','space'}, dimensions={0} | all-to-all | bytes 1441792 | tf_op jit(solution)/shard_map/all_to_all | solution.py:423
  22.1 0.0 copy-done
  22.1 0.0 copy-done.3
  22.1 1.0 %shard_map.83 = (f32[3,8,8,128]{3,2,1,0:T(8,128)S(1)}, f32[4,5,8,8,128]{4,3,2,1,0:T(8,128)S(1)}, f32[4,8,128]{2,1,0:T(8,128)S(1)}, f32[8,8,128]{2,1,0:T(8,128)S(1)}) custom-call(f32[16,88,128]{2,1,0:T(8,128)S(1)} %all_to_all.10.got_ref, f32[128,128]{1,0:T(8,128)S(1)} %copy-done, f32[1,128]{1,0:T(1,128)S(1)} %copy-done.3), custom_call_target="tpu_custom_call" | custom-call | tf_op jit(solution)/shard_map/pallas_call | solution.py:425
  23.0 3.5 %collective-permute-start = (f32[3,8,8,128]{3,2,1,0:T(8,128)S(1)}, f32[3,8,8,128]{3,2,1,0:T(8,128)S(1)}, u32[]{:S(2)}, u32[]{:S(2)}) collective-permute-start(f32[3,8,8,128]{3,2,1,0:T(8,128)S(1)} %get-tuple-element.18), channel_id=1, source_target_pairs={{0,16},{1,17},{2,18},{3,19},{4,20},{5,21},{6,22},{7,23},{8,24},{9,... | collective-permute-start | bytes 294920 | tf_op jit(solution)/shard_map/ppermute | solution.py:431
  26.6 1.1 %shard_map.84 = (f32[4,5,8,8,128]{4,3,2,1,0:T(8,128)S(1)}, f32[4,8,128]{2,1,0:T(8,128)S(1)}, f32[16,80,128]{2,1,0:T(8,128)S(1)}) custom-call(f32[16,88,128]{2,1,0:T(8,128)S(1)} %all_to_all.10.got_ref, f32[4,5,8,8,128]{4,3,2,1,0:T(8,128)S(1)} %get-tuple-element.12.modes_in, ...), custom_call_target="tpu_custom_call", output_to_operand_aliasing={{0}: (1, {}), {1}: (2, {})} | custom-call | tf_op jit(solution)/shard_map/pallas_call | solution.py:433
  27.6 1.1 %collective-permute-done.came_ref = f32[3,8,8,128]{3,2,1,0:T(8,128)S(1)} collective-permute-done((f32[3,8,8,128]{3,2,1,0:T(8,128)S(1)}, f32[3,8,8,128]{3,2,1,0:T(8,128)S(1)}, u32[]{:S(2)}, u32[]{:S(2)}) %collective-permute-start) | collective-permute-done | bytes 98336 | tf_op jit(solution)/shard_map/ppermute | solution.py:431
  28.7 0.0 copy-start.1
  28.7 0.0 copy-start.2
  28.8 16.0 %all_to_all.11.got_ref = f32[16,80,128]{2,1,0:T(8,128)S(1)} all-to-all(f32[16,80,128]{2,1,0:T(8,128)S(1)} %shard_map.85), channel_id=1, replica_groups=mesh['hi'=2,'lo'=4,'space'=4] {'lo','space'}, dimensions={0} | all-to-all | bytes 1310720 | tf_op jit(solution)/shard_map/all_to_all | solution.py:452
  44.8 0.0 copy-done.1
  44.8 0.0 copy-done.2
  44.8 1.4 %shard_map.86 = f32[1,5,2,128,128]{4,3,2,1,0:T(8,128)} custom-call(f32[16,80,128]{2,1,0:T(8,128)S(1)} %all_to_all.11.got_ref, bf16[256,256]{1,0:T(8,128)(2,1)S(1)} %copy-done.2, bf16[256,256]{1,0:T(8,128)(2,1)S(1)} %copy-done.1), custom_call_target="tpu_custom_call" | custom-call | tf_op jit(solution)/shard_map/pallas_call | solution.py:453
  (1 shorter events, 0.0 us)
Async XLA Ops:
  3.2 18.9 %copy-start = (f32[128,128]{1,0:T(8,128)S(1)}, f32[128,128]{1,0:T(8,128)}, u32[]{:S(2)}) copy-start(f32[128,128]{1,0:T(8,128)} %constant.10.clone.x_ref) | copy-start | bytes 196612
  3.2 18.9 %copy-start.3 = (f32[1,128]{1,0:T(1,128)S(1)}, f32[1,128]{1,0:T(1,128)}, u32[]{:S(2)}) copy-start(f32[1,128]{1,0:T(1,128)} %constant.11.clone.y_ref) | copy-start | bytes 1540
  23.0 5.7 %collective-permute-start = (f32[3,8,8,128]{3,2,1,0:T(8,128)S(1)}, f32[3,8,8,128]{3,2,1,0:T(8,128)S(1)}, u32[]{:S(2)}, u32[]{:S(2)}) collective-permute-start(f32[3,8,8,128]{3,2,1,0:T(8,128)S(1)} %get-tuple-element.18), channel_id=1, source_target_pairs={{0,16},{1,17},{2,18},{3,19},{4,20},{5,21},{6,22},{7,23},{8,24},{9,... | collective-permute-start | bytes 294920 | tf_op jit(solution)/shard_map/ppermute | solution.py:431
  28.7 16.0 %copy-start.1 = (bf16[256,256]{1,0:T(8,128)(2,1)S(1)}, bf16[256,256]{1,0:T(8,128)(2,1)}, u32[]{:S(2)}) copy-start(bf16[256,256]{1,0:T(8,128)(2,1)} %constant.9.clone.left_hbm.left_ref) | copy-start | bytes 393220
  28.7 16.0 %copy-start.2 = (bf16[256,256]{1,0:T(8,128)(2,1)S(1)}, bf16[256,256]{1,0:T(8,128)(2,1)}, u32[]{:S(2)}) copy-start(bf16[256,256]{1,0:T(8,128)(2,1)} %constant.8.clone.right_hbm.right_ref) | copy-start | bytes 393220

commit v4 on v3

v4 whole, which is shorter than its diff:
```python
import functools
import math

import jax
import jax.numpy as jnp
import numpy as np
from jax import lax
from jax.experimental import pallas as pl
from jax.experimental.pallas import tpu as pltpu
from jax.sharding import Mesh
from jax.sharding import PartitionSpec as P

TILE = 8


def node_tables():
    radical = math.sqrt(3.0 / 7.0)
    node_times = [0.0, (1.0 - radical) / 2.0, 0.5, (1.0 + radical) / 2.0, 1.0]
    integrals = np.zeros((4, 5))
    for column in range(5):
        coeffs = [1.0]
        for other_index in range(5):
            if other_index == column:
                continue
            other_time = node_times[other_index]
            scaling = node_times[column] - other_time
            grown = [0.0] * (len(coeffs) + 1)
            for exponent in range(len(coeffs)):
                grown[exponent + 1] += coeffs[exponent] / scaling
                grown[exponent] -= coeffs[exponent] * other_time / scaling
            coeffs = grown
        for section in range(4):
            integrals[section, column] = sum(
                coeffs[exponent]
                * (node_times[section + 1] ** (exponent + 1) - node_times[section] ** (exponent + 1))
                / (exponent + 1)
                for exponent in range(len(coeffs))
            )
    coarse = [0.0, 0.5, 1.0]
    interp = np.zeros((5, 3))
    for column in range(3):
        for section in range(5):
            weight = 1.0
            for other_index in range(3):
                if other_index != column:
                    weight = (
                        weight
                        * (node_times[section] - coarse[other_index])
                        / (coarse[column] - coarse[other_index])
                    )
            interp[section, column] = weight
    return (np.array(node_times), integrals, interp)


TIMES, QUAD, INTERP = node_tables()
SPACING = np.diff(TIMES)
LEFT = QUAD[0] + QUAD[1]
RIGHT = QUAD[2] + QUAD[3]


def sine(length):
    index = np.arange(1, length + 1)
    return math.sqrt(2.0 / (length + 1)) * np.sin(math.pi / (length + 1) * np.outer(index, index))


def eigen(length):
    return 2.0 - 2.0 * np.cos(math.pi / (length + 1) * np.arange(1, length + 1))


def sine_parts(length):
    matrix = sine(length)
    high = matrix.astype(jnp.bfloat16)
    low = (matrix - high.astype(np.float64)).astype(jnp.bfloat16)
    return np.stack([high, low])


def right_table(length):
    high, low = sine_parts(length)
    return np.block([[high, low], [high, np.zeros_like(high)]])


def left_table(length):
    high, low = sine_parts(length)
    return np.block([[high, high], [low, np.zeros_like(high)]])


def split(value):
    high = value.astype(jnp.bfloat16)
    return high, (value - high.astype(jnp.float32)).astype(jnp.bfloat16)


def times_sine(value, table):
    width = value.shape[-1]
    both = jnp.dot(
        jnp.concatenate(split(value), axis=1), table, preferred_element_type=jnp.float32
    )
    return both[:, :width] + both[:, width:]


def sine_times(value, table):
    width = value.shape[0]
    both = jnp.dot(
        table, jnp.concatenate(split(value), axis=0), preferred_element_type=jnp.float32
    )
    return both[:width] + both[width:]


def sine_list(values):
    count = len(values)
    matrix = sine(count)
    half = count // 2
    even = [values[i] + values[count - 1 - i] for i in range(half)]
    odd = [values[i] - values[count - 1 - i] for i in range(half)]
    middle = [values[half]] if count % 2 else []
    result = []
    for k in range(count):
        terms = even + middle if k % 2 == 0 else odd
        result.append(sum(float(matrix[k, i]) * term for i, term in enumerate(terms)))
    return result


def zero(value):
    return isinstance(value, float) and value == 0.0


def plus(*values):
    values = [v for v in values if not zero(v)]
    return sum(values[1:], values[0]) if values else 0.0


def times(factor, value):
    return 0.0 if zero(factor) or zero(value) else factor * value


def minus(value, other):
    return value if zero(other) else plus(value, -other)


def combine(weights, values):
    return plus(*(times(float(w), v) for w, v in zip(weights, values)))


def sweep(first, nodes, forced, scaled):
    swept = [first]
    for m in range(4):
        inner = combine(QUAD[m], nodes)
        if m:
            inner = plus(inner, times(float(SPACING[m]), minus(swept[m], nodes[m])))
        swept.append(plus(swept[m], times(scaled, inner), forced[m]))
    left = plus(times(scaled, combine(LEFT - 0.5 * np.eye(5)[0], swept)), *forced[:2])
    right = plus(times(scaled, combine(RIGHT - 0.5 * np.eye(5)[2], swept)), *forced[2:])
    return swept, left, right


def chain(start, left, right, gain):
    middle = plus(times(gain, start), left)
    return middle, plus(times(gain, middle), right)


def correct(swept, start, middle, ending):
    deltas = [minus(start, swept[0]), minus(middle, swept[2]), minus(ending, swept[4])]
    return [
        start,
        plus(swept[1], combine(INTERP[1], deltas)),
        middle,
        plus(swept[3], combine(INTERP[3], deltas)),
        ending,
    ]


def march(guesses, forced, scaled, state, final):
    before, first, second = state
    fields = []
    for j, guess in enumerate(guesses):
        gain = 1.0 + 0.5 * scaled[j]
        swept, left, right = sweep(before, [before] + [guess] * 4, forced[j], scaled[j])
        middle, ending = chain(first, left, right, gain)
        nodes = correct(swept, first, middle, ending)
        swept, left, right = sweep(first, nodes, forced[j], scaled[j])
        middle, last = chain(second, left, right, gain)
        if final:
            fields.append(correct(swept, second, middle, last))
        before, first, second = guess, ending, last
    return fields if final else (before, first, second)


def responses(scaled):
    nothing = [0.0] * len(scaled)
    return [
        march(nothing, [[0.0] * 4] * len(scaled), scaled, [float(i == k) for k in range(3)], True)
        for i in range(3)
    ]


def distinct(lo):
    return [(j, m) for j in range(lo) for m in range(5) if j == 0 or m]


def forward_kernel(
    dims, step_ref, init_hbm, guess_hbm, forcing_hbm, parts_hbm, out_ref,
    init_ref, guess_ref, forcing_ref, parts_ref, table_ref, sems, plane_sems,
):
    depth, groups, per, lo, space = dims[:5]
    pieces = lo // depth
    copies = [
        pltpu.make_async_copy(parts_hbm, parts_ref, sems.at[0]),
        pltpu.make_async_copy(init_hbm, init_ref, sems.at[1]),
        pltpu.make_async_copy(guess_hbm.at[0], guess_ref, sems.at[2]),
    ]
    copies += [
        pltpu.make_async_copy(forcing_hbm.at[0, :, d], forcing_ref.at[d], plane_sems.at[d])
        for d in range(depth)
    ]
    for copy in copies:
        copy.start()
    step = step_ref[0]
    width = parts_ref.shape[1]

    copies[0].wait()
    high, low = parts_ref[0], parts_ref[1]
    table_ref[:width, :width] = high
    table_ref[:width, width:] = high
    table_ref[width:, :width] = low
    table_ref[width:, width:] = jnp.zeros_like(low)

    def transform(planes):
        joined = sine_times(jnp.concatenate(planes, axis=1), table_ref[...])
        half = joined.shape[1] // len(planes)
        return [
            joined[:, i * half : (i + 1) * half].reshape(groups, per, half)
            for i in range(len(planes))
        ]

    def put(field, d, tiles):
        row = (field * depth + d) * per
        out_ref[:, row : row + per, :] = tiles

    copies[1].wait()
    starts = transform([init_ref[d] for d in range(depth)])
    mine = lax.axis_index("lo")
    rows = per // pieces
    share = None
    for i in range(lo):
        offset = (i % pieces) * rows
        tile = starts[i // pieces][:, offset : offset + rows]
        share = tile if share is None else jnp.where(mine == i, tile, share)
    base = 5 * depth * per
    out_ref[:, base : base + rows, :] = share
    out_ref[:, base + rows :, :] = jnp.full(
        (groups, out_ref.shape[1] - base - rows, out_ref.shape[2]), step, jnp.float32
    )
    copies[2].wait()
    for d, tiles in enumerate(transform([guess_ref[d] for d in range(depth)])):
        put(0, d, tiles)
    for d in range(depth):
        copies[3 + d].wait()
        samples = [forcing_ref[d, j] for j in range(5)]
        for m in (0, 2):
            pair = [step * combine(QUAD[k], samples) for k in (m, m + 1)]
            for k, tiles in enumerate(transform(pair)):
                put(1 + m + k, d, tiles)


def source(dims, j, z):
    depth, groups, per, lo, space, cores = dims
    device = z // depth
    return (device % cores * lo + j) * (space // cores) + device // cores, z % depth


def to_modes(dims, got_ref, right_ref, modes_ref, steps_ref):
    depth, groups, per, lo, space, cores = dims
    base = 5 * depth * per + per // (lo // depth)
    count = depth * space
    for j in range(lo):
        columns = []
        for f in range(5):
            tiles = []
            for z in range(count):
                device, d = source(dims, j, z)
                row = (f * depth + d) * per
                tiles.append(got_ref[device, row : row + per, :])
            columns += sine_list(tiles)
        mixed = times_sine(jnp.concatenate(columns, axis=0), right_ref[...])
        modes_ref[j] = mixed.reshape(5, count, per, mixed.shape[1])
        steps_ref[j] = jnp.broadcast_to(
            got_ref[source(dims, j, 0)[0], base : base + 1, :], steps_ref.shape[1:]
        )


def initial_modes(dims, got_ref, right_ref):
    depth, groups, per, lo, space, cores = dims
    pieces = lo // depth
    base = 5 * depth * per
    rows = per // pieces
    tiles = []
    for z in range(depth * space):
        first = (z % depth) * pieces
        parts = [
            got_ref[source(dims, i, z)[0], base : base + rows, :]
            for i in range(first, first + pieces)
        ]
        tiles.append(jnp.concatenate(parts, axis=0))
    mixed = times_sine(jnp.concatenate(sine_list(tiles), axis=0), right_ref[...])
    return mixed.reshape(depth * space, per, mixed.shape[1])


def per_mode(dims, modes_ref, steps_ref, x_ref, y_ref):
    depth, groups, per, lo, space, cores = dims
    device = lax.axis_index("core") * lo + lax.axis_index("lo")
    owner = device * (space // cores) + lax.axis_index("chip")
    plane = x_ref[pl.ds(owner * per, per), :] + y_ref[...]
    steps = [steps_ref[j] for j in range(lo)]
    for z, weight in enumerate(eigen(depth * space)):
        neg = -(plane + float(weight))
        guesses = [modes_ref[j, 0, z] for j in range(lo)]
        forced = [[modes_ref[j, 1 + m, z] for m in range(4)] for j in range(lo)]
        yield z, guesses, forced, [s * neg for s in steps]


def put_fields(dims, fields_of, out_ref):
    depth, groups, per, lo, space, cores = dims
    for j, m in distinct(lo):
        for z, tile in enumerate(sine_list(fields_of(j, m))):
            places = [(j, m)] + ([(j + 1, 0)] if m == 4 and j + 1 < lo else [])
            for slot, node in places:
                device, d = source(dims, slot, z)
                row = (node * depth + d) * per
                out_ref[device, row : row + per, :] = tile


def first_kernel(
    dims, got_ref, right_ref, x_ref, y_ref, state_ref, modes_ref, steps_ref, start_ref
):
    @pl.when(lax.axis_index("hi") == 0)
    def _():
        to_modes(dims, got_ref, right_ref, modes_ref, steps_ref)
        start_ref[...] = initial_modes(dims, got_ref, right_ref)
        for z, guesses, forced, scaled in per_mode(dims, modes_ref, steps_ref, x_ref, y_ref):
            state = march(guesses, forced, scaled, (start_ref[z],) * 3, False)
            for i in range(3):
                state_ref[i, z] = state[i]


def window_kernel(
    dims, got_ref, modes_in, steps_in, start_ref, right_ref, x_ref, y_ref,
    modes_ref, steps_ref, out_ref, part_ref, unit_ref,
):
    depth, groups, per, lo, space, cores = dims
    head = lax.axis_index("hi") == 0

    @pl.when(head)
    def _():
        for z, guesses, forced, scaled in per_mode(dims, modes_ref, steps_ref, x_ref, y_ref):
            fields = march(guesses, forced, scaled, (start_ref[z],) * 3, True)
            for k, (j, m) in enumerate(distinct(lo)):
                part_ref[k, z] = fields[j][m]
        where = {place: k for k, place in enumerate(distinct(lo))}
        put_fields(
            dims,
            lambda j, m: [part_ref[where[j, m], z] for z in range(depth * space)],
            out_ref,
        )

    @pl.when(jnp.logical_not(head))
    def _():
        to_modes(dims, got_ref, right_ref, modes_ref, steps_ref)
        for z, guesses, forced, scaled in per_mode(dims, modes_ref, steps_ref, x_ref, y_ref):
            fields = march(guesses, forced, scaled, (0.0,) * 3, True)
            added = responses(scaled)
            for k, (j, m) in enumerate(distinct(lo)):
                if not zero(fields[j][m]):
                    part_ref[k, z] = fields[j][m]
                for i in range(3):
                    if not isinstance(added[i][j][m], float):
                        unit_ref[i, k, z] = added[i][j][m]


def middle_kernel(dims, state_in, modes_ref, steps_ref, came_ref, x_ref, y_ref, state_ref):
    @pl.when(lax.axis_index("hi") > 0)
    def _():
        for z, guesses, forced, scaled in per_mode(dims, modes_ref, steps_ref, x_ref, y_ref):
            came = tuple(came_ref[i, z] for i in range(3))
            state = march(guesses, forced, scaled, came, False)
            for i in range(3):
                state_ref[i, z] = state[i]


def finish_kernel(dims, out_in, part_ref, unit_ref, came_ref, out_ref):
    depth, groups, per, lo, space, cores = dims

    @pl.when(lax.axis_index("hi") > 0)
    def _():
        stand = [np.float32(0.5)] * lo
        fields = march(stand, [stand[:1] * 4] * lo, stand, (0.0,) * 3, True)
        added = responses(stand)
        where = {place: k for k, place in enumerate(distinct(lo))}

        def fields_of(j, m):
            k = where[j, m]
            tiles = []
            for z in range(depth * space):
                terms = [] if zero(fields[j][m]) else [part_ref[k, z]]
                for i in range(3):
                    unit = added[i][j][m]
                    if not isinstance(unit, float):
                        unit = unit_ref[i, k, z]
                    terms.append(times(unit, came_ref[i, z]))
                tiles.append(plus(*terms))
            return tiles

        put_fields(dims, fields_of, out_ref)


def backward_kernel(dims, got_ref, right_ref, left_ref, out_hbm, out_ref, sems):
    depth, groups, per = dims[:3]
    rows, width = got_ref.shape[1:]
    copies = []
    for i in range(0, 5 * depth, 2):
        mixed = times_sine(
            got_ref[:, i * per : (i + 2) * per, :].reshape(groups * 2 * per, width), right_ref[...]
        ).reshape(groups, 2 * per, width)
        pair = jnp.concatenate(
            [
                mixed[:, :per].reshape(groups * per, width),
                mixed[:, per:].reshape(groups * per, width),
            ],
            axis=1,
        )
        pair = sine_times(pair, left_ref[...])
        for k, plane in ((i, pair[:, :width]), (i + 1, pair[:, width:])):
            out_ref[k] = plane
            copy = pltpu.make_async_copy(
                out_ref.at[k], out_hbm.at[0, k // depth, k % depth], sems.at[k]
            )
            copy.start()
            copies.append(copy)
    for copy in copies:
        copy.wait()


VMEM = pl.BlockSpec(memory_space=pltpu.VMEM)
SMEM = pl.BlockSpec(memory_space=pltpu.SMEM)
HBM = pl.BlockSpec(memory_space=pltpu.HBM)


def in_hbm(value):
    return pltpu.with_memory_space_constraint(value, pltpu.HBM)


def call(kernel, shapes, in_specs, scratch=(), out_spec=VMEM, aliases=None):
    return pl.pallas_call(
        kernel,
        out_shape=[jax.ShapeDtypeStruct(s, jnp.float32) for s in shapes],
        in_specs=in_specs,
        out_specs=[out_spec] * len(shapes),
        scratch_shapes=list(scratch),
        input_output_aliases=aliases or {},
        compiler_params=pltpu.CompilerParams(vmem_limit_bytes=12 * 2**20),
    )


def body(initial, start_guess, forcing, step_size):
    depth, width_x, width_y = initial.shape
    hi, lo, chips, cores = (lax.axis_size(a) for a in ("hi", "lo", "chip", "core"))
    space = chips * cores
    groups = space * lo
    per = width_x // groups
    dims = (depth, groups, per, lo, space, cores)
    count = depth * space
    parts = jnp.asarray(sine_parts(width_x))
    right = jnp.asarray(right_table(width_y))
    left = jnp.asarray(left_table(width_x))
    x_weights = jnp.asarray(
        np.broadcast_to(eigen(width_x)[:, None], (width_x, width_y)).astype(np.float32)
    )
    y_weights = jnp.asarray(eigen(width_y)[None, :].astype(np.float32))
    tile = (per, width_y)
    plane = (width_x, width_y)
    bind = functools.partial

    rows = 5 * depth * per
    (send,) = call(
        bind(forward_kernel, dims),
        [(groups, rows + TILE, width_y)],
        [SMEM] + [HBM] * 4,
        [
            pltpu.VMEM((depth, *plane), jnp.float32),
            pltpu.VMEM((depth, *plane), jnp.float32),
            pltpu.VMEM((depth, 5, *plane), jnp.float32),
            pltpu.VMEM(parts.shape, parts.dtype),
            pltpu.VMEM(left.shape, left.dtype),
            pltpu.SemaphoreType.DMA((3,)),
            pltpu.SemaphoreType.DMA((depth,)),
        ],
    )(step_size, *(in_hbm(a) for a in (initial, start_guess, forcing, parts)))
    members = ("core", "lo", "chip")
    got = lax.all_to_all(send, members, 0, 0, tiled=True)
    state_shape, modes_shape, steps_shape = (3, count, *tile), (lo, 5, count, *tile), (lo, *tile)
    state, modes, steps, start = call(
        bind(first_kernel, dims),
        [state_shape, modes_shape, steps_shape, (count, *tile)],
        [VMEM] * 4,
    )(got, right, x_weights, y_weights)
    onward = [(i, i + 1) for i in range(hi - 1)]
    came = lax.ppermute(state, "hi", onward)
    kinds = len(distinct(lo))
    modes, steps, send, part, unit = call(
        bind(window_kernel, dims),
        [
            modes_shape,
            steps_shape,
            (groups, rows, width_y),
            (kinds, count, *tile),
            (3, kinds, count, *tile),
        ],
        [VMEM] * 7,
        aliases={1: 0, 2: 1},
    )(got, modes, steps, start, right, x_weights, y_weights)
    for _ in range(hi - 2):
        (state,) = call(bind(middle_kernel, dims), [state_shape], [VMEM] * 6, aliases={0: 0})(
            state, modes, steps, came, x_weights, y_weights
        )
        came = lax.ppermute(state, "hi", onward)
    (send,) = call(
        bind(finish_kernel, dims), [(groups, rows, width_y)], [VMEM] * 4, aliases={0: 0}
    )(send, part, unit, came)
    got = lax.all_to_all(send, members, 0, 0, tiled=True)
    (fields,) = call(
        bind(backward_kernel, dims),
        [(1, 5, depth, width_x, width_y)],
        [VMEM] * 3,
        [
            pltpu.VMEM((5 * depth, *plane), jnp.float32),
            pltpu.SemaphoreType.DMA((5 * depth,)),
        ],
        HBM,
    )(got, right, left)
    return fields


def solution(mesh):
    steps, space = mesh.devices.shape
    cores = 2 if space % 2 == 0 else 1
    time, slabs = ("hi", "lo"), ("chip", "core")
    specs = (P(slabs), P(time, slabs), P(time, None, slabs), P(time))

    def run(initial, start_guess, forcing, step_size):
        width = initial.shape[1]
        lo = max(
            d for d in range(1, steps + 1) if steps % d == 0 and width % (TILE * d * space) == 0
        )
        shape = (steps // lo, lo, space // cores, cores)
        whole = Mesh(mesh.devices.reshape(shape), time + slabs)
        return jax.shard_map(
            body, mesh=whole, in_specs=specs, out_specs=P(time, None, slabs), check_vma=False
        )(initial, start_guess, forcing, step_size)

    return run
```

time: 46.9 us -> 45.6 us (0.972)
  blocking collectives: 34.9 us -> 34.4 us
    all_to_all x2, blocking collectives: 34.9 us -> 34.4 us  [body(): got = lax.all_to_all(send, members, 0, 0, tiled=True)]
where the time goes in v4:
time: 45.6 us; the launch traced here: 45.3 us
  blocking collectives  34.4 us (75%)
  Pallas kernels  5.72 us (13%)
  starting transfers between devices  3.33 us (7%)
  waiting for transfers between devices  1.12 us (2%)
  between operations  0.73 us (2%)
    all_to_all x2, blocking collectives, body(): got = lax.all_to_all(send, members, 0, 0, tiled=True)  34.4 us
    ppermute x1, starting transfers between devices, body(): came = lax.ppermute(state, 'hi', onward)  3.33 us
    pallas_call x1, Pallas kernels, body(): call(bind(forward_kernel, dims), [(groups, rows + TILE, width_y)], [SMEM]...  2.03 us
    pallas_call x1, Pallas kernels, body(): call(bind(backward_kernel, dims), [(1, 5, depth, width_x, width_y)], [VME...  1.43 us
    pallas_call x1, Pallas kernels, body(): call(bind(first_kernel, dims), [state_shape, modes_shape, steps_shape, (c...  1.19 us
    ppermute x1, waiting for transfers between devices, body(): came = lax.ppermute(state, 'hi', onward)  1.12 us
    pallas_call x1, Pallas kernels, body(): call(bind(window_kernel, dims), [modes_shape, steps_shape, (groups, rows,...  1.06 us
  transfers between devices with their start and end apart: 1, of which 1 were waited for; matrix products, arithmetic and copies ran while one was open for 0% of the time, Pallas kernels for 2%

profile of v4, /device:TPU:0, one launch (start us, length us, event | category | flops | bytes accessed | tf_op | source)
XLA Modules:
  0.0 45.3 jit_solution(14772247700534035310)
XLA Ops:
  0.0 0.0 copy-start
  0.0 0.0 copy-start.3
  0.0 0.0 copy-start.1
  0.7 2.0 %shard_map.91 = f32[16,88,128]{2,1,0:T(8,128)S(1)} custom-call(f32[1]{0:T(128)S(6)} %copy.16.step_ref, f32[2,128,128]{2,1,0:T(8,128)} %init_hbm.1, f32[1,2,128,128]{3,2,1,0:T(8,128)} %guess_hbm.1, f32[1,5,2,128,128]{4,3,2,1,0:T(8,128)} %forcing_hbm.1, bf16[2,128,128]{2,1,0:T(8,128)(2,1)} %constant.10.clone.parts_hbm), custom_call_target="tpu_custom_call" | custom-call | tf_op jit(solution)/shard_map/pallas_call | solution.py:482
  2.7 18.5 %all_to_all.10.got_ref = f32[16,88,128]{2,1,0:T(8,128)S(1)} all-to-all(f32[16,88,128]{2,1,0:T(8,128)S(1)} %shard_map.91), channel_id=1, replica_groups=mesh['hi'=2,'lo'=4,'chip'=2,'core'=2] {'core','lo','chip'}, dimensions={0} | all-to-all | bytes 1441792 | tf_op jit(solution)/shard_map/all_to_all | solution.py:497
  21.3 0.0 copy-done
  21.3 0.0 copy-done.3
  21.3 0.0 copy-done.1
  21.3 1.2 %shard_map.92 = (f32[3,8,8,128]{3,2,1,0:T(8,128)S(1)}, f32[4,5,8,8,128]{4,3,2,1,0:T(8,128)S(1)}, f32[4,8,128]{2,1,0:T(8,128)S(1)}, f32[8,8,128]{2,1,0:T(8,128)S(1)}) custom-call(f32[16,88,128]{2,1,0:T(8,128)S(1)} %all_to_all.10.got_ref, bf16[256,256]{1,0:T(8,128)(2,1)S(1)} %copy-done, f32[128,128]{1,0:T(8,128)S(1)} %copy-done.1, f32[1,128]{1,0:T(1,128)S(1)} %copy-done.3), custom_call_target="tpu_custom_call" | custom-call | tf_op jit(solution)/shard_map/pallas_call | solution.py:499
  22.5 3.3 %collective-permute-start = (f32[3,8,8,128]{3,2,1,0:T(8,128)S(1)}, f32[3,8,8,128]{3,2,1,0:T(8,128)S(1)}, u32[]{:S(2)}, u32[]{:S(2)}) collective-permute-start(f32[3,8,8,128]{3,2,1,0:T(8,128)S(1)} %get-tuple-element.18), channel_id=1, source_target_pairs={{0,16},{1,17},{2,18},{3,19},{4,20},{5,21},{6,22},{7,23},{8,24},{9,... | collective-permute-start | bytes 294920 | tf_op jit(solution)/shard_map/ppermute | solution.py:505
  25.8 1.1 %shard_map.93 = (f32[4,5,8,8,128]{4,3,2,1,0:T(8,128)S(1)}, f32[4,8,128]{2,1,0:T(8,128)S(1)}, f32[16,80,128]{2,1,0:T(8,128)S(1)}, f32[17,8,8,128]{3,2,1,0:T(8,128)S(1)}, f32[3,17,8,8,128]{4,3,2,1,0:T(8,128)S(1)}) custom-call(f32[16,88,128]{2,1,0:T(8,128)S(1)} %all_to_all.10.got_ref, ...), custom_call_target="tpu_custom_call", output_to_operand_aliasing={{0}: (1, {}), {1}: (2, {})} | custom-call | tf_op jit(solution)/shard_map/pallas_call | solution.py:507
  26.9 1.1 %collective-permute-done.came_ref = f32[3,8,8,128]{3,2,1,0:T(8,128)S(1)} collective-permute-done((f32[3,8,8,128]{3,2,1,0:T(8,128)S(1)}, f32[3,8,8,128]{3,2,1,0:T(8,128)S(1)}, u32[]{:S(2)}, u32[]{:S(2)}) %collective-permute-start) | collective-permute-done | bytes 98336 | tf_op jit(solution)/shard_map/ppermute | solution.py:505
  28.0 0.0 copy-start.2
  28.0 15.9 %all_to_all.11.got_ref = f32[16,80,128]{2,1,0:T(8,128)S(1)} all-to-all(f32[16,80,128]{2,1,0:T(8,128)S(1)} %shard_map.94), channel_id=1, replica_groups=mesh['hi'=2,'lo'=4,'chip'=2,'core'=2] {'core','lo','chip'}, dimensions={0} | all-to-all | bytes 1310720 | tf_op jit(solution)/shard_map/all_to_all | solution.py:527
  43.9 0.0 copy-done.2
  43.9 1.4 %shard_map.95 = f32[1,5,2,128,128]{4,3,2,1,0:T(8,128)} custom-call(f32[16,80,128]{2,1,0:T(8,128)S(1)} %all_to_all.11.got_ref, bf16[256,256]{1,0:T(8,128)(2,1)S(1)} %copy-done, bf16[256,256]{1,0:T(8,128)(2,1)S(1)} %copy-done.2), custom_call_target="tpu_custom_call" | custom-call | tf_op jit(solution)/shard_map/pallas_call | solution.py:528
  (1 shorter events, 0.0 us)
Async XLA Ops:
  0.0 21.3 %copy-start = (bf16[256,256]{1,0:T(8,128)(2,1)S(1)}, bf16[256,256]{1,0:T(8,128)(2,1)}, u32[]{:S(2)}) copy-start(bf16[256,256]{1,0:T(8,128)(2,1)} %constant.11.clone.right_ref) | copy-start | bytes 393220
  0.0 21.3 %copy-start.3 = (f32[1,128]{1,0:T(1,128)S(1)}, f32[1,128]{1,0:T(1,128)}, u32[]{:S(2)}) copy-start(f32[1,128]{1,0:T(1,128)} %constant.14.clone.y_ref) | copy-start | bytes 1540
  0.0 21.3 %copy-start.1 = (f32[128,128]{1,0:T(8,128)S(1)}, f32[128,128]{1,0:T(8,128)}, u32[]{:S(2)}) copy-start(f32[128,128]{1,0:T(8,128)} %constant.13.clone.x_ref) | copy-start | bytes 196612
  22.5 5.5 %collective-permute-start = (f32[3,8,8,128]{3,2,1,0:T(8,128)S(1)}, f32[3,8,8,128]{3,2,1,0:T(8,128)S(1)}, u32[]{:S(2)}, u32[]{:S(2)}) collective-permute-start(f32[3,8,8,128]{3,2,1,0:T(8,128)S(1)} %get-tuple-element.18), channel_id=1, source_target_pairs={{0,16},{1,17},{2,18},{3,19},{4,20},{5,21},{6,22},{7,23},{8,24},{9,... | collective-permute-start | bytes 294920 | tf_op jit(solution)/shard_map/ppermute | solution.py:505
  28.0 15.9 %copy-start.2 = (bf16[256,256]{1,0:T(8,128)(2,1)S(1)}, bf16[256,256]{1,0:T(8,128)(2,1)}, u32[]{:S(2)}) copy-start(bf16[256,256]{1,0:T(8,128)(2,1)} %constant.12.clone.left_ref) | copy-start | bytes 393220

commit v5 on v4

--- a/solution.py
+++ b/solution.py
@@ -216,7 +216,8 @@
     step = step_ref[0]
     width = parts_ref.shape[1]
 
-    copies[0].wait()
+    for copy in copies:
+        copy.wait()
     high, low = parts_ref[0], parts_ref[1]
     table_ref[:width, :width] = high
     table_ref[:width, width:] = high
@@ -235,7 +236,6 @@
         row = (field * depth + d) * per
         out_ref[:, row : row + per, :] = tiles
 
-    copies[1].wait()
     starts = transform([init_ref[d] for d in range(depth)])
     mine = lax.axis_index("lo")
     rows = per // pieces
@@ -249,11 +249,9 @@
     out_ref[:, base + rows :, :] = jnp.full(
         (groups, out_ref.shape[1] - base - rows, out_ref.shape[2]), step, jnp.float32
     )
-    copies[2].wait()
     for d, tiles in enumerate(transform([guess_ref[d] for d in range(depth)])):
         put(0, d, tiles)
     for d in range(depth):
-        copies[3 + d].wait()
         samples = [forcing_ref[d, j] for j in range(5)]
         for m in (0, 2):
             pair = [step * combine(QUAD[k], samples) for k in (m, m + 1)]
@@ -317,15 +315,22 @@
         yield z, guesses, forced, [s * neg for s in steps]
 
 
-def put_fields(dims, fields_of, out_ref):
-    depth, groups, per, lo, space, cores = dims
-    for j, m in distinct(lo):
-        for z, tile in enumerate(sine_list(fields_of(j, m))):
+def put_fields(dims, fields_of, right_ref, out_ref):
+    depth, groups, per, lo, space, cores = dims
+    for j in range(lo):
+        nodes = range(5) if j == 0 else range(1, 5)
+        columns = []
+        for m in nodes:
+            columns += sine_list(fields_of(j, m))
+        mixed = times_sine(jnp.concatenate(columns, axis=0), right_ref[...])
+        for k, m in enumerate(nodes):
             places = [(j, m)] + ([(j + 1, 0)] if m == 4 and j + 1 < lo else [])
-            for slot, node in places:
-                device, d = source(dims, slot, z)
-                row = (node * depth + d) * per
-                out_ref[device, row : row + per, :] = tile
+            for z in range(depth * space):
+                first = (k * depth * space + z) * per
+                for slot, node in places:
+                    device, d = source(dims, slot, z)
+                    row = (node * depth + d) * per
+                    out_ref[device, row : row + per, :] = mixed[first : first + per]
 
 
 def first_kernel(
@@ -358,6 +363,7 @@
         put_fields(
             dims,
             lambda j, m: [part_ref[where[j, m], z] for z in range(depth * space)],
+            right_ref,
             out_ref,
         )
 
@@ -385,7 +391,7 @@
                 state_ref[i, z] = state[i]
 
 
-def finish_kernel(dims, out_in, part_ref, unit_ref, came_ref, out_ref):
+def finish_kernel(dims, out_in, part_ref, unit_ref, came_ref, right_ref, out_ref):
     depth, groups, per, lo, space, cores = dims
 
     @pl.when(lax.axis_index("hi") > 0)
@@ -408,21 +414,18 @@
                 tiles.append(plus(*terms))
             return tiles
 
-        put_fields(dims, fields_of, out_ref)
-
-
-def backward_kernel(dims, got_ref, right_ref, left_ref, out_hbm, out_ref, sems):
+        put_fields(dims, fields_of, right_ref, out_ref)
+
+
+def backward_kernel(dims, got_ref, left_ref, out_hbm, out_ref, sems):
     depth, groups, per = dims[:3]
-    rows, width = got_ref.shape[1:]
+    width = got_ref.shape[2]
     copies = []
     for i in range(0, 5 * depth, 2):
-        mixed = times_sine(
-            got_ref[:, i * per : (i + 2) * per, :].reshape(groups * 2 * per, width), right_ref[...]
-        ).reshape(groups, 2 * per, width)
         pair = jnp.concatenate(
             [
-                mixed[:, :per].reshape(groups * per, width),
-                mixed[:, per:].reshape(groups * per, width),
+                got_ref[:, k * per : (k + 1) * per, :].reshape(groups * per, width)
+                for k in (i, i + 1)
             ],
             axis=1,
         )
@@ -522,19 +525,19 @@
         )
         came = lax.ppermute(state, "hi", onward)
     (send,) = call(
-        bind(finish_kernel, dims), [(groups, rows, width_y)], [VMEM] * 4, aliases={0: 0}
-    )(send, part, unit, came)
+        bind(finish_kernel, dims), [(groups, rows, width_y)], [VMEM] * 5, aliases={0: 0}
+    )(send, part, unit, came, right)
     got = lax.all_to_all(send, members, 0, 0, tiled=True)
     (fields,) = call(
         bind(backward_kernel, dims),
         [(1, 5, depth, width_x, width_y)],
-        [VMEM] * 3,
+        [VMEM] * 2,
         [
             pltpu.VMEM((5 * depth, *plane), jnp.float32),
             pltpu.SemaphoreType.DMA((5 * depth,)),
         ],
         HBM,
-    )(got, right, left)
+    )(got, left)
     return fields
 
 

time: 45.6 us -> 45 us (0.987)
  transfers between devices with their start and end apart: 1 -> 1, of which waited for: 1 -> 1; matrix products, arithmetic and copies ran while one was open for 0% -> 0% of each run, Pallas kernels for 2% -> 3%
where the time goes in v5:
time: 45 us; the launch traced here: 44.8 us
  blocking collectives  34.4 us (76%)
  Pallas kernels  5.39 us (12%)
  starting transfers between devices  3.35 us (7%)
  waiting for transfers between devices  0.88 us (2%)
  between operations  0.73 us (2%)
    all_to_all x2, blocking collectives, body(): got = lax.all_to_all(send, members, 0, 0, tiled=True)  34.4 us
    ppermute x1, starting transfers between devices, body(): came = lax.ppermute(state, 'hi', onward)  3.35 us
    pallas_call x1, Pallas kernels, body(): call(bind(forward_kernel, dims), [(groups, rows + TILE, width_y)], [SMEM]...  1.77 us
    pallas_call x1, Pallas kernels, body(): call(bind(window_kernel, dims), [modes_shape, steps_shape, (groups, rows,...  1.31 us
    pallas_call x1, Pallas kernels, body(): call(bind(first_kernel, dims), [state_shape, modes_shape, steps_shape, (c...  1.17 us
    pallas_call x1, Pallas kernels, body(): call(bind(backward_kernel, dims), [(1, 5, depth, width_x, width_y)], [VME...  1.14 us
  transfers between devices with their start and end apart: 1, of which 1 were waited for; matrix products, arithmetic and copies ran while one was open for 0% of the time, Pallas kernels for 3%

profile of v5, /device:TPU:0, one launch (start us, length us, event | category | flops | bytes accessed | tf_op | source)
XLA Modules:
  0.0 44.8 jit_solution(10466909291789474017)
XLA Ops:
  0.0 0.0 copy-start
  0.0 0.0 copy-start.3
  0.0 0.0 copy-start.1
  0.7 1.8 %shard_map.91 = f32[16,88,128]{2,1,0:T(8,128)S(1)} custom-call(f32[1]{0:T(128)S(6)} %copy.16.step_ref, f32[2,128,128]{2,1,0:T(8,128)} %init_hbm.1, f32[1,2,128,128]{3,2,1,0:T(8,128)} %guess_hbm.1, f32[1,5,2,128,128]{4,3,2,1,0:T(8,128)} %forcing_hbm.1, bf16[2,128,128]{2,1,0:T(8,128)(2,1)} %constant.10.clone.parts_hbm), custom_call_target="tpu_custom_call" | custom-call | tf_op jit(solution)/shard_map/pallas_call | solution.py:485
  2.5 18.5 %all_to_all.10.got_ref = f32[16,88,128]{2,1,0:T(8,128)S(1)} all-to-all(f32[16,88,128]{2,1,0:T(8,128)S(1)} %shard_map.91), channel_id=1, replica_groups=mesh['hi'=2,'lo'=4,'chip'=2,'core'=2] {'core','lo','chip'}, dimensions={0} | all-to-all | bytes 1441792 | tf_op jit(solution)/shard_map/all_to_all | solution.py:500
  21.0 0.0 copy-done
  21.0 0.0 copy-done.3
  21.0 0.0 copy-done.1
  21.0 1.2 %shard_map.92 = (f32[3,8,8,128]{3,2,1,0:T(8,128)S(1)}, f32[4,5,8,8,128]{4,3,2,1,0:T(8,128)S(1)}, f32[4,8,128]{2,1,0:T(8,128)S(1)}, f32[8,8,128]{2,1,0:T(8,128)S(1)}) custom-call(f32[16,88,128]{2,1,0:T(8,128)S(1)} %all_to_all.10.got_ref, bf16[256,256]{1,0:T(8,128)(2,1)S(1)} %copy-done, f32[128,128]{1,0:T(8,128)S(1)} %copy-done.1, f32[1,128]{1,0:T(1,128)S(1)} %copy-done.3), custom_call_target="tpu_custom_call" | custom-call | tf_op jit(solution)/shard_map/pallas_call | solution.py:502
  22.2 3.4 %collective-permute-start = (f32[3,8,8,128]{3,2,1,0:T(8,128)S(1)}, f32[3,8,8,128]{3,2,1,0:T(8,128)S(1)}, u32[]{:S(2)}, u32[]{:S(2)}) collective-permute-start(f32[3,8,8,128]{3,2,1,0:T(8,128)S(1)} %get-tuple-element.18), channel_id=1, source_target_pairs={{0,16},{1,17},{2,18},{3,19},{4,20},{5,21},{6,22},{7,23},{8,24},{9,... | collective-permute-start | bytes 294920 | tf_op jit(solution)/shard_map/ppermute | solution.py:508
  25.5 1.3 %shard_map.93 = (f32[4,5,8,8,128]{4,3,2,1,0:T(8,128)S(1)}, f32[4,8,128]{2,1,0:T(8,128)S(1)}, f32[16,80,128]{2,1,0:T(8,128)S(1)}, f32[17,8,8,128]{3,2,1,0:T(8,128)S(1)}, f32[3,17,8,8,128]{4,3,2,1,0:T(8,128)S(1)}) custom-call(f32[16,88,128]{2,1,0:T(8,128)S(1)} %all_to_all.10.got_ref, ...), custom_call_target="tpu_custom_call", output_to_operand_aliasing={{0}: (1, {}), {1}: (2, {})} | custom-call | tf_op jit(solution)/shard_map/pallas_call | solution.py:510
  26.8 0.9 %collective-permute-done.came_ref = f32[3,8,8,128]{3,2,1,0:T(8,128)S(1)} collective-permute-done((f32[3,8,8,128]{3,2,1,0:T(8,128)S(1)}, f32[3,8,8,128]{3,2,1,0:T(8,128)S(1)}, u32[]{:S(2)}, u32[]{:S(2)}) %collective-permute-start) | collective-permute-done | bytes 98336 | tf_op jit(solution)/shard_map/ppermute | solution.py:508
  27.7 0.0 copy-start.2
  27.7 15.9 %all_to_all.11.got_ref = f32[16,80,128]{2,1,0:T(8,128)S(1)} all-to-all(f32[16,80,128]{2,1,0:T(8,128)S(1)} %shard_map.94), channel_id=1, replica_groups=mesh['hi'=2,'lo'=4,'chip'=2,'core'=2] {'core','lo','chip'}, dimensions={0} | all-to-all | bytes 1310720 | tf_op jit(solution)/shard_map/all_to_all | solution.py:530
  43.6 0.0 copy-done.2
  43.6 1.1 %shard_map.95 = f32[1,5,2,128,128]{4,3,2,1,0:T(8,128)} custom-call(f32[16,80,128]{2,1,0:T(8,128)S(1)} %all_to_all.11.got_ref, bf16[256,256]{1,0:T(8,128)(2,1)S(1)} %copy-done.2), custom_call_target="tpu_custom_call" | custom-call | tf_op jit(solution)/shard_map/pallas_call | solution.py:531
  (1 shorter events, 0.0 us)
Async XLA Ops:
  0.0 21.0 %copy-start = (bf16[256,256]{1,0:T(8,128)(2,1)S(1)}, bf16[256,256]{1,0:T(8,128)(2,1)}, u32[]{:S(2)}) copy-start(bf16[256,256]{1,0:T(8,128)(2,1)} %constant.11.clone.right_ref) | copy-start | bytes 393220
  0.0 21.0 %copy-start.3 = (f32[1,128]{1,0:T(1,128)S(1)}, f32[1,128]{1,0:T(1,128)}, u32[]{:S(2)}) copy-start(f32[1,128]{1,0:T(1,128)} %constant.14.clone.y_ref) | copy-start | bytes 1540
  0.0 21.0 %copy-start.1 = (f32[128,128]{1,0:T(8,128)S(1)}, f32[128,128]{1,0:T(8,128)}, u32[]{:S(2)}) copy-start(f32[128,128]{1,0:T(8,128)} %constant.13.clone.x_ref) | copy-start | bytes 196612
  22.2 5.6 %collective-permute-start = (f32[3,8,8,128]{3,2,1,0:T(8,128)S(1)}, f32[3,8,8,128]{3,2,1,0:T(8,128)S(1)}, u32[]{:S(2)}, u32[]{:S(2)}) collective-permute-start(f32[3,8,8,128]{3,2,1,0:T(8,128)S(1)} %get-tuple-element.18), channel_id=1, source_target_pairs={{0,16},{1,17},{2,18},{3,19},{4,20},{5,21},{6,22},{7,23},{8,24},{9,... | collective-permute-start | bytes 294920 | tf_op jit(solution)/shard_map/ppermute | solution.py:508
  27.7 15.9 %copy-start.2 = (bf16[256,256]{1,0:T(8,128)(2,1)S(1)}, bf16[256,256]{1,0:T(8,128)(2,1)}, u32[]{:S(2)}) copy-start(bf16[256,256]{1,0:T(8,128)(2,1)} %constant.12.clone.left_ref) | copy-start | bytes 393220

commit v6 on v5

--- a/solution.py
+++ b/solution.py
@@ -11,6 +11,7 @@
 from jax.sharding import PartitionSpec as P
 
 TILE = 8
+COST = 10**10
 
 
 def node_tables():
@@ -196,33 +197,21 @@
     return [(j, m) for j in range(lo) for m in range(5) if j == 0 or m]
 
 
+def blank_kernel(out_ref):
+    out_ref[...] = jnp.zeros(out_ref.shape, out_ref.dtype)
+
+
 def forward_kernel(
-    dims, step_ref, init_hbm, guess_hbm, forcing_hbm, parts_hbm, out_ref,
-    init_ref, guess_ref, forcing_ref, parts_ref, table_ref, sems, plane_sems,
+    dims, step_ref, init_ref, guess_ref, forcing_ref, parts_ref, blank_ref, out_ref, table_ref
 ):
     depth, groups, per, lo, space = dims[:5]
     pieces = lo // depth
-    copies = [
-        pltpu.make_async_copy(parts_hbm, parts_ref, sems.at[0]),
-        pltpu.make_async_copy(init_hbm, init_ref, sems.at[1]),
-        pltpu.make_async_copy(guess_hbm.at[0], guess_ref, sems.at[2]),
-    ]
-    copies += [
-        pltpu.make_async_copy(forcing_hbm.at[0, :, d], forcing_ref.at[d], plane_sems.at[d])
-        for d in range(depth)
-    ]
-    for copy in copies:
-        copy.start()
-    step = step_ref[0]
     width = parts_ref.shape[1]
-
-    for copy in copies:
-        copy.wait()
     high, low = parts_ref[0], parts_ref[1]
     table_ref[:width, :width] = high
     table_ref[:width, width:] = high
     table_ref[width:, :width] = low
-    table_ref[width:, width:] = jnp.zeros_like(low)
+    table_ref[width:, width:] = blank_ref[...]
 
     def transform(planes):
         joined = sine_times(jnp.concatenate(planes, axis=1), table_ref[...])
@@ -244,15 +233,16 @@
         offset = (i % pieces) * rows
         tile = starts[i // pieces][:, offset : offset + rows]
         share = tile if share is None else jnp.where(mine == i, tile, share)
+    step = step_ref[0]
     base = 5 * depth * per
     out_ref[:, base : base + rows, :] = share
     out_ref[:, base + rows :, :] = jnp.full(
         (groups, out_ref.shape[1] - base - rows, out_ref.shape[2]), step, jnp.float32
     )
-    for d, tiles in enumerate(transform([guess_ref[d] for d in range(depth)])):
+    for d, tiles in enumerate(transform([guess_ref[0, d] for d in range(depth)])):
         put(0, d, tiles)
     for d in range(depth):
-        samples = [forcing_ref[d, j] for j in range(5)]
+        samples = [forcing_ref[0, j, d] for j in range(5)]
         for m in (0, 2):
             pair = [step * combine(QUAD[k], samples) for k in (m, m + 1)]
             for k, tiles in enumerate(transform(pair)):
@@ -446,10 +436,6 @@
 HBM = pl.BlockSpec(memory_space=pltpu.HBM)
 
 
-def in_hbm(value):
-    return pltpu.with_memory_space_constraint(value, pltpu.HBM)
-
-
 def call(kernel, shapes, in_specs, scratch=(), out_spec=VMEM, aliases=None):
     return pl.pallas_call(
         kernel,
@@ -482,20 +468,20 @@
     bind = functools.partial
 
     rows = 5 * depth * per
+    extra = -(-(per // (lo // depth) + 1) // TILE) * TILE
+    blank = pl.pallas_call(
+        blank_kernel,
+        out_shape=jax.ShapeDtypeStruct((width_x, width_x), parts.dtype),
+        out_specs=VMEM,
+        cost_estimate=pl.CostEstimate(flops=COST, bytes_accessed=COST, transcendentals=0),
+        compiler_params=pltpu.CompilerParams(vmem_limit_bytes=2**20),
+    )()
     (send,) = call(
         bind(forward_kernel, dims),
-        [(groups, rows + TILE, width_y)],
-        [SMEM] + [HBM] * 4,
-        [
-            pltpu.VMEM((depth, *plane), jnp.float32),
-            pltpu.VMEM((depth, *plane), jnp.float32),
-            pltpu.VMEM((depth, 5, *plane), jnp.float32),
-            pltpu.VMEM(parts.shape, parts.dtype),
-            pltpu.VMEM(left.shape, left.dtype),
-            pltpu.SemaphoreType.DMA((3,)),
-            pltpu.SemaphoreType.DMA((depth,)),
-        ],
-    )(step_size, *(in_hbm(a) for a in (initial, start_guess, forcing, parts)))
+        [(groups, rows + extra, width_y)],
+        [SMEM] + [VMEM] * 5,
+        [pltpu.VMEM(left.shape, left.dtype)],
+    )(step_size, initial, start_guess, forcing, parts, blank)
     members = ("core", "lo", "chip")
     got = lax.all_to_all(send, members, 0, 0, tiled=True)
     state_shape, modes_shape, steps_shape = (3, count, *tile), (lo, 5, count, *tile), (lo, *tile)

time: 45 us -> 44.2 us (0.982)
  Pallas kernels: 5.39 us -> 4.14 us
    pallas_call x1 -> x2, Pallas kernels: 1.77 us -> 0.52 us  [the longest x1 0.52 us: body(): call(bind(forward_kernel, dims), [(groups, rows + extra, width_y)], [SMEM...]
where the time goes in v6:
time: 44.2 us; the launch traced here: 44 us
  blocking collectives  34.4 us (78%)
  Pallas kernels  4.14 us (9%)
  starting transfers between devices  3.36 us (8%)
  waiting for transfers between devices  0.88 us (2%)
  between operations  0.8 us (2%)
    all_to_all x2, blocking collectives, body(): got = lax.all_to_all(send, members, 0, 0, tiled=True)  34.4 us
    ppermute x1, starting transfers between devices, body(): came = lax.ppermute(state, 'hi', onward)  3.36 us
    pallas_call x1, Pallas kernels, body(): call(bind(window_kernel, dims), [modes_shape, steps_shape, (groups, rows,...  1.31 us
    pallas_call x1, Pallas kernels, body(): call(bind(first_kernel, dims), [state_shape, modes_shape, steps_shape, (c...  1.17 us
    pallas_call x1, Pallas kernels, body(): call(bind(backward_kernel, dims), [(1, 5, depth, width_x, width_y)], [VME...  1.14 us
  transfers between devices with their start and end apart: 1, of which 1 were waited for; matrix products, arithmetic and copies ran while one was open for 0% of the time, Pallas kernels for 3%

profile of v6, /device:TPU:0, one launch (start us, length us, event | category | flops | bytes accessed | tf_op | source)
XLA Modules:
  0.0 44.0 jit_solution(8534974329425728768)
XLA Ops:
  0.0 0.0 copy-start.6
  0.0 0.0 copy-start.1
  0.0 0.0 copy-start.4
  0.0 0.0 copy-start.3
  0.0 0.0 copy-start
  0.0 0.0 copy-start.2
  0.0 0.0 copy-start.7
  0.8 0.0 copy-done.6
  0.8 0.3 copy-done.1
  1.1 0.0 copy-done.4
  1.2 0.0 copy-done.3
  1.2 0.5 %shard_map.92 = f32[16,88,128]{2,1,0:T(8,128)S(1)} custom-call(f32[1]{0:T(128)S(6)} %copy.16.step_ref, f32[2,128,128]{2,1,0:T(8,128)S(1)} %copy-done.3, f32[1,2,128,128]{3,2,1,0:T(8,128)S(1)} %copy-done.4, f32[1,5,2,128,128]{4,3,2,1,0:T(8,128)S(1)} %copy-done.1, bf16[2,128,128]{2,1,0:T(8,128)(2,1)S(1)} %copy-done.6, bf16[128,128]{1,0:T(8,128)(2,1)S(1)} %shard_map.91.blank_ref), custom_call_target="tpu_custom_call" | custom-call | tf_op jit(solution)/shard_map/pallas_call | solution.py:479
  1.7 18.5 %all_to_all.10.got_ref = f32[16,88,128]{2,1,0:T(8,128)S(1)} all-to-all(f32[16,88,128]{2,1,0:T(8,128)S(1)} %shard_map.92), channel_id=1, replica_groups=mesh['hi'=2,'lo'=4,'chip'=2,'core'=2] {'core','lo','chip'}, dimensions={0} | all-to-all | bytes 1441792 | tf_op jit(solution)/shard_map/all_to_all | solution.py:486
  20.2 0.0 copy-done
  20.2 0.0 copy-done.2
  20.2 0.0 copy-done.7
  20.2 1.2 %shard_map.93 = (f32[3,8,8,128]{3,2,1,0:T(8,128)S(1)}, f32[4,5,8,8,128]{4,3,2,1,0:T(8,128)S(1)}, f32[4,8,128]{2,1,0:T(8,128)S(1)}, f32[8,8,128]{2,1,0:T(8,128)S(1)}) custom-call(f32[16,88,128]{2,1,0:T(8,128)S(1)} %all_to_all.10.got_ref, bf16[256,256]{1,0:T(8,128)(2,1)S(1)} %copy-done, f32[128,128]{1,0:T(8,128)S(1)} %copy-done.2, f32[1,128]{1,0:T(1,128)S(1)} %copy-done.7), custom_call_target="tpu_custom_call" | custom-call | tf_op jit(solution)/shard_map/pallas_call | solution.py:488
  21.4 3.4 %collective-permute-start = (f32[3,8,8,128]{3,2,1,0:T(8,128)S(1)}, f32[3,8,8,128]{3,2,1,0:T(8,128)S(1)}, u32[]{:S(2)}, u32[]{:S(2)}) collective-permute-start(f32[3,8,8,128]{3,2,1,0:T(8,128)S(1)} %get-tuple-element.18), channel_id=1, source_target_pairs={{0,16},{1,17},{2,18},{3,19},{4,20},{5,21},{6,22},{7,23},{8,24},{9,... | collective-permute-start | bytes 294920 | tf_op jit(solution)/shard_map/ppermute | solution.py:494
  24.8 1.3 %shard_map.94 = (f32[4,5,8,8,128]{4,3,2,1,0:T(8,128)S(1)}, f32[4,8,128]{2,1,0:T(8,128)S(1)}, f32[16,80,128]{2,1,0:T(8,128)S(1)}, f32[17,8,8,128]{3,2,1,0:T(8,128)S(1)}, f32[3,17,8,8,128]{4,3,2,1,0:T(8,128)S(1)}) custom-call(f32[16,88,128]{2,1,0:T(8,128)S(1)} %all_to_all.10.got_ref, ...), custom_call_target="tpu_custom_call", output_to_operand_aliasing={{0}: (1, {}), {1}: (2, {})} | custom-call | tf_op jit(solution)/shard_map/pallas_call | solution.py:496
  26.1 0.9 %collective-permute-done.came_ref = f32[3,8,8,128]{3,2,1,0:T(8,128)S(1)} collective-permute-done((f32[3,8,8,128]{3,2,1,0:T(8,128)S(1)}, f32[3,8,8,128]{3,2,1,0:T(8,128)S(1)}, u32[]{:S(2)}, u32[]{:S(2)}) %collective-permute-start) | collective-permute-done | bytes 98336 | tf_op jit(solution)/shard_map/ppermute | solution.py:494
  27.0 0.0 copy-start.5
  27.0 15.9 %all_to_all.11.got_ref = f32[16,80,128]{2,1,0:T(8,128)S(1)} all-to-all(f32[16,80,128]{2,1,0:T(8,128)S(1)} %shard_map.95), channel_id=1, replica_groups=mesh['hi'=2,'lo'=4,'chip'=2,'core'=2] {'core','lo','chip'}, dimensions={0} | all-to-all | bytes 1310720 | tf_op jit(solution)/shard_map/all_to_all | solution.py:516
  42.9 0.0 copy-done.5
  42.9 1.1 %shard_map.96 = f32[1,5,2,128,128]{4,3,2,1,0:T(8,128)} custom-call(f32[16,80,128]{2,1,0:T(8,128)S(1)} %all_to_all.11.got_ref, bf16[256,256]{1,0:T(8,128)(2,1)S(1)} %copy-done.5), custom_call_target="tpu_custom_call" | custom-call | tf_op jit(solution)/shard_map/pallas_call | solution.py:517
  (2 shorter events, 0.0 us)
Async XLA Ops:
  0.0 0.8 %copy-start.6 = (bf16[2,128,128]{2,1,0:T(8,128)(2,1)S(1)}, bf16[2,128,128]{2,1,0:T(8,128)(2,1)}, u32[]{:S(2)}) copy-start(bf16[2,128,128]{2,1,0:T(8,128)(2,1)} %constant.10.clone.parts_ref) | copy-start | bytes 196612
  0.0 1.1 %copy-start.1 = (f32[1,5,2,128,128]{4,3,2,1,0:T(8,128)S(1)}, f32[1,5,2,128,128]{4,3,2,1,0:T(8,128)}, u32[]{:S(2)}) copy-start(f32[1,5,2,128,128]{4,3,2,1,0:T(8,128)} %forcing_ref.1) | copy-start | bytes 1966084
  0.0 1.2 %copy-start.4 = (f32[1,2,128,128]{3,2,1,0:T(8,128)S(1)}, f32[1,2,128,128]{3,2,1,0:T(8,128)}, u32[]{:S(2)}) copy-start(f32[1,2,128,128]{3,2,1,0:T(8,128)} %guess_ref.1) | copy-start | bytes 393220
  0.0 1.2 %copy-start.3 = (f32[2,128,128]{2,1,0:T(8,128)S(1)}, f32[2,128,128]{2,1,0:T(8,128)}, u32[]{:S(2)}) copy-start(f32[2,128,128]{2,1,0:T(8,128)} %init_ref.1) | copy-start | bytes 393220
  0.0 20.2 %copy-start = (bf16[256,256]{1,0:T(8,128)(2,1)S(1)}, bf16[256,256]{1,0:T(8,128)(2,1)}, u32[]{:S(2)}) copy-start(bf16[256,256]{1,0:T(8,128)(2,1)} %constant.11.clone.right_ref) | copy-start | bytes 393220
  0.0 20.2 %copy-start.2 = (f32[128,128]{1,0:T(8,128)S(1)}, f32[128,128]{1,0:T(8,128)}, u32[]{:S(2)}) copy-start(f32[128,128]{1,0:T(8,128)} %constant.13.clone.x_ref) | copy-start | bytes 196612
  0.0 20.2 %copy-start.7 = (f32[1,128]{1,0:T(1,128)S(1)}, f32[1,128]{1,0:T(1,128)}, u32[]{:S(2)}) copy-start(f32[1,128]{1,0:T(1,128)} %constant.14.clone.y_ref) | copy-start | bytes 1540
  21.4 5.6 %collective-permute-start = (f32[3,8,8,128]{3,2,1,0:T(8,128)S(1)}, f32[3,8,8,128]{3,2,1,0:T(8,128)S(1)}, u32[]{:S(2)}, u32[]{:S(2)}) collective-permute-start(f32[3,8,8,128]{3,2,1,0:T(8,128)S(1)} %get-tuple-element.18), channel_id=1, source_target_pairs={{0,16},{1,17},{2,18},{3,19},{4,20},{5,21},{6,22},{7,23},{8,24},{9,... | collective-permute-start | bytes 294920 | tf_op jit(solution)/shard_map/ppermute | solution.py:494
  27.0 15.9 %copy-start.5 = (bf16[256,256]{1,0:T(8,128)(2,1)S(1)}, bf16[256,256]{1,0:T(8,128)(2,1)}, u32[]{:S(2)}) copy-start(bf16[256,256]{1,0:T(8,128)(2,1)} %constant.12.clone.left_ref) | copy-start | bytes 393220

commit v7 on v6

--- a/solution.py
+++ b/solution.py
@@ -490,8 +490,9 @@
         [state_shape, modes_shape, steps_shape, (count, *tile)],
         [VMEM] * 4,
     )(got, right, x_weights, y_weights)
-    onward = [(i, i + 1) for i in range(hi - 1)]
-    came = lax.ppermute(state, "hi", onward)
+    onward = [(i, i + lo) for i in range((hi - 1) * lo)]
+    onward += [((hi - 1) * lo + i, (i + lo // 2) % lo) for i in range(lo)]
+    came = lax.ppermute(state, ("hi", "lo"), onward)
     kinds = len(distinct(lo))
     modes, steps, send, part, unit = call(
         bind(window_kernel, dims),
@@ -509,7 +510,7 @@
         (state,) = call(bind(middle_kernel, dims), [state_shape], [VMEM] * 6, aliases={0: 0})(
             state, modes, steps, came, x_weights, y_weights
         )
-        came = lax.ppermute(state, "hi", onward)
+        came = lax.ppermute(state, ("hi", "lo"), onward)
     (send,) = call(
         bind(finish_kernel, dims), [(groups, rows, width_y)], [VMEM] * 5, aliases={0: 0}
     )(send, part, unit, came, right)

time: 44.2 us -> 43.8 us (level)
  waiting for transfers between devices: 0.88 us -> 3.67 us
  starting transfers between devices: 3.36 us -> 1.5 us
  blocking collectives: 34.4 us -> 33 us
    ppermute x1, waiting for transfers between devices: 0.88 us -> 3.67 us  [body(): came = lax.ppermute(state, ('hi', 'lo'), onward)]
    ppermute x1, starting transfers between devices: 3.36 us -> 1.5 us  [body(): came = lax.ppermute(state, ('hi', 'lo'), onward)]
    all_to_all x2, blocking collectives: 34.4 us -> 33 us  [body(): got = lax.all_to_all(send, members, 0, 0, tiled=True)]
where the time goes in v7:
time: 43.8 us; the launch traced here: 43.5 us
  blocking collectives  33 us (75%)
  Pallas kernels  4.13 us (9%)
  waiting for transfers between devices  3.67 us (8%)
  starting transfers between devices  1.5 us (3%)
  between operations  0.79 us (2%)
    all_to_all x2, blocking collectives, body(): got = lax.all_to_all(send, members, 0, 0, tiled=True)  33 us
    ppermute x1, waiting for transfers between devices, body(): came = lax.ppermute(state, ('hi', 'lo'), onward)  3.67 us
    ppermute x1, starting transfers between devices, body(): came = lax.ppermute(state, ('hi', 'lo'), onward)  1.5 us
    pallas_call x1, Pallas kernels, body(): call(bind(window_kernel, dims), [modes_shape, steps_shape, (groups, rows,...  1.29 us
    pallas_call x1, Pallas kernels, body(): call(bind(first_kernel, dims), [state_shape, modes_shape, steps_shape, (c...  1.17 us
    pallas_call x1, Pallas kernels, body(): call(bind(backward_kernel, dims), [(1, 5, depth, width_x, width_y)], [VME...  1.14 us
  transfers between devices with their start and end apart: 1, of which 1 were waited for; matrix products, arithmetic and copies ran while one was open for 0% of the time, Pallas kernels for 3%

profile of v7, /device:TPU:0, one launch (start us, length us, event | category | flops | bytes accessed | tf_op | source)
XLA Modules:
  0.0 43.5 jit_solution(9398564323290740786)
XLA Ops:
  0.0 0.0 copy-start.6
  0.0 0.0 copy-start.1
  0.0 0.0 copy-start.4
  0.0 0.0 copy-start.3
  0.0 0.0 copy-start
  0.0 0.0 copy-start.2
  0.0 0.0 copy-start.7
  0.8 0.0 copy-done.6
  0.8 0.3 copy-done.1
  1.1 0.0 copy-done.4
  1.2 0.0 copy-done.3
  1.2 0.5 %shard_map.92 = f32[16,88,128]{2,1,0:T(8,128)S(1)} custom-call(f32[1]{0:T(128)S(6)} %copy.16.step_ref, f32[2,128,128]{2,1,0:T(8,128)S(1)} %copy-done.3, f32[1,2,128,128]{3,2,1,0:T(8,128)S(1)} %copy-done.4, f32[1,5,2,128,128]{4,3,2,1,0:T(8,128)S(1)} %copy-done.1, bf16[2,128,128]{2,1,0:T(8,128)(2,1)S(1)} %copy-done.6, bf16[128,128]{1,0:T(8,128)(2,1)S(1)} %shard_map.91.blank_ref), custom_call_target="tpu_custom_call" | custom-call | tf_op jit(solution)/shard_map/pallas_call | solution.py:479
  1.7 18.5 %all_to_all.10.got_ref = f32[16,88,128]{2,1,0:T(8,128)S(1)} all-to-all(f32[16,88,128]{2,1,0:T(8,128)S(1)} %shard_map.92), channel_id=1, replica_groups=mesh['hi'=2,'lo'=4,'chip'=2,'core'=2] {'core','lo','chip'}, dimensions={0} | all-to-all | bytes 1441792 | tf_op jit(solution)/shard_map/all_to_all | solution.py:486
  20.2 0.0 copy-done
  20.2 0.0 copy-done.2
  20.2 0.0 copy-done.7
  20.2 1.2 %shard_map.93 = (f32[3,8,8,128]{3,2,1,0:T(8,128)S(1)}, f32[4,5,8,8,128]{4,3,2,1,0:T(8,128)S(1)}, f32[4,8,128]{2,1,0:T(8,128)S(1)}, f32[8,8,128]{2,1,0:T(8,128)S(1)}) custom-call(f32[16,88,128]{2,1,0:T(8,128)S(1)} %all_to_all.10.got_ref, bf16[256,256]{1,0:T(8,128)(2,1)S(1)} %copy-done, f32[128,128]{1,0:T(8,128)S(1)} %copy-done.2, f32[1,128]{1,0:T(1,128)S(1)} %copy-done.7), custom_call_target="tpu_custom_call" | custom-call | tf_op jit(solution)/shard_map/pallas_call | solution.py:488
  21.4 1.5 %collective-permute-start = (f32[3,8,8,128]{3,2,1,0:T(8,128)S(1)}, f32[3,8,8,128]{3,2,1,0:T(8,128)S(1)}, u32[]{:S(2)}, u32[]{:S(2)}) collective-permute-start(f32[3,8,8,128]{3,2,1,0:T(8,128)S(1)} %get-tuple-element.18), channel_id=1, source_target_pairs={{0,16},{4,20},{8,24},{12,28},{16,8},{20,12},{24,0},{28,4},{1,17},{... | collective-permute-start | bytes 294920 | tf_op jit(solution)/shard_map/ppermute | solution.py:495
  22.9 1.3 %shard_map.94 = (f32[4,5,8,8,128]{4,3,2,1,0:T(8,128)S(1)}, f32[4,8,128]{2,1,0:T(8,128)S(1)}, f32[16,80,128]{2,1,0:T(8,128)S(1)}, f32[17,8,8,128]{3,2,1,0:T(8,128)S(1)}, f32[3,17,8,8,128]{4,3,2,1,0:T(8,128)S(1)}) custom-call(f32[16,88,128]{2,1,0:T(8,128)S(1)} %all_to_all.10.got_ref, ...), custom_call_target="tpu_custom_call", output_to_operand_aliasing={{0}: (1, {}), {1}: (2, {})} | custom-call | tf_op jit(solution)/shard_map/pallas_call | solution.py:497
  24.2 3.7 %collective-permute-done.came_ref = f32[3,8,8,128]{3,2,1,0:T(8,128)S(1)} collective-permute-done((f32[3,8,8,128]{3,2,1,0:T(8,128)S(1)}, f32[3,8,8,128]{3,2,1,0:T(8,128)S(1)}, u32[]{:S(2)}, u32[]{:S(2)}) %collective-permute-start) | collective-permute-done | bytes 98336 | tf_op jit(solution)/shard_map/ppermute | solution.py:495
  27.9 0.0 copy-start.5
  27.9 14.5 %all_to_all.11.got_ref = f32[16,80,128]{2,1,0:T(8,128)S(1)} all-to-all(f32[16,80,128]{2,1,0:T(8,128)S(1)} %shard_map.95), channel_id=1, replica_groups=mesh['hi'=2,'lo'=4,'chip'=2,'core'=2] {'core','lo','chip'}, dimensions={0} | all-to-all | bytes 1310720 | tf_op jit(solution)/shard_map/all_to_all | solution.py:517
  42.4 0.0 copy-done.5
  42.4 1.1 %shard_map.96 = f32[1,5,2,128,128]{4,3,2,1,0:T(8,128)} custom-call(f32[16,80,128]{2,1,0:T(8,128)S(1)} %all_to_all.11.got_ref, bf16[256,256]{1,0:T(8,128)(2,1)S(1)} %copy-done.5), custom_call_target="tpu_custom_call" | custom-call | tf_op jit(solution)/shard_map/pallas_call | solution.py:518
  (2 shorter events, 0.0 us)
Async XLA Ops:
  0.0 0.8 %copy-start.6 = (bf16[2,128,128]{2,1,0:T(8,128)(2,1)S(1)}, bf16[2,128,128]{2,1,0:T(8,128)(2,1)}, u32[]{:S(2)}) copy-start(bf16[2,128,128]{2,1,0:T(8,128)(2,1)} %constant.10.clone.parts_ref) | copy-start | bytes 196612
  0.0 1.1 %copy-start.1 = (f32[1,5,2,128,128]{4,3,2,1,0:T(8,128)S(1)}, f32[1,5,2,128,128]{4,3,2,1,0:T(8,128)}, u32[]{:S(2)}) copy-start(f32[1,5,2,128,128]{4,3,2,1,0:T(8,128)} %forcing_ref.1) | copy-start | bytes 1966084
  0.0 1.2 %copy-start.4 = (f32[1,2,128,128]{3,2,1,0:T(8,128)S(1)}, f32[1,2,128,128]{3,2,1,0:T(8,128)}, u32[]{:S(2)}) copy-start(f32[1,2,128,128]{3,2,1,0:T(8,128)} %guess_ref.1) | copy-start | bytes 393220
  0.0 1.2 %copy-start.3 = (f32[2,128,128]{2,1,0:T(8,128)S(1)}, f32[2,128,128]{2,1,0:T(8,128)}, u32[]{:S(2)}) copy-start(f32[2,128,128]{2,1,0:T(8,128)} %init_ref.1) | copy-start | bytes 393220
  0.0 20.2 %copy-start = (bf16[256,256]{1,0:T(8,128)(2,1)S(1)}, bf16[256,256]{1,0:T(8,128)(2,1)}, u32[]{:S(2)}) copy-start(bf16[256,256]{1,0:T(8,128)(2,1)} %constant.11.clone.right_ref) | copy-start | bytes 393220
  0.0 20.2 %copy-start.2 = (f32[128,128]{1,0:T(8,128)S(1)}, f32[128,128]{1,0:T(8,128)}, u32[]{:S(2)}) copy-start(f32[128,128]{1,0:T(8,128)} %constant.13.clone.x_ref) | copy-start | bytes 196612
  0.0 20.2 %copy-start.7 = (f32[1,128]{1,0:T(1,128)S(1)}, f32[1,128]{1,0:T(1,128)}, u32[]{:S(2)}) copy-start(f32[1,128]{1,0:T(1,128)} %constant.14.clone.y_ref) | copy-start | bytes 1540
  21.4 6.5 %collective-permute-start = (f32[3,8,8,128]{3,2,1,0:T(8,128)S(1)}, f32[3,8,8,128]{3,2,1,0:T(8,128)S(1)}, u32[]{:S(2)}, u32[]{:S(2)}) collective-permute-start(f32[3,8,8,128]{3,2,1,0:T(8,128)S(1)} %get-tuple-element.18), channel_id=1, source_target_pairs={{0,16},{4,20},{8,24},{12,28},{16,8},{20,12},{24,0},{28,4},{1,17},{... | collective-permute-start | bytes 294920 | tf_op jit(solution)/shard_map/ppermute | solution.py:495
  27.9 14.5 %copy-start.5 = (bf16[256,256]{1,0:T(8,128)(2,1)S(1)}, bf16[256,256]{1,0:T(8,128)(2,1)}, u32[]{:S(2)}) copy-start(bf16[256,256]{1,0:T(8,128)(2,1)} %constant.12.clone.left_ref) | copy-start | bytes 393220

commit v8 on v7

--- a/solution.py
+++ b/solution.py
@@ -138,18 +138,24 @@
 
 
 def combine(weights, values):
-    return plus(*(times(float(w), v) for w, v in zip(weights, values)))
+    merged = {}
+    for weight, value in zip(weights, values):
+        known = merged.get(id(value), (0.0, value))
+        merged[id(value)] = (known[0] + float(weight), value)
+    return plus(*(times(w, v) for w, v in merged.values()))
 
 
 def sweep(first, nodes, forced, scaled):
+    unit = np.eye(5)
     swept = [first]
     for m in range(4):
-        inner = combine(QUAD[m], nodes)
+        weights = QUAD[m] - (SPACING[m] * unit[m] if m else 0.0)
+        inner = combine(weights, nodes)
         if m:
-            inner = plus(inner, times(float(SPACING[m]), minus(swept[m], nodes[m])))
+            inner = plus(inner, times(float(SPACING[m]), swept[m]))
         swept.append(plus(swept[m], times(scaled, inner), forced[m]))
-    left = plus(times(scaled, combine(LEFT - 0.5 * np.eye(5)[0], swept)), *forced[:2])
-    right = plus(times(scaled, combine(RIGHT - 0.5 * np.eye(5)[2], swept)), *forced[2:])
+    left = plus(times(scaled, combine(LEFT - 0.5 * unit[0], swept)), *forced[:2])
+    right = plus(times(scaled, combine(RIGHT - 0.5 * unit[2], swept)), *forced[2:])
     return swept, left, right
 
 

time: 43.8 us -> 43.7 us (level)
  no operation moved by 1% of the time
where the time goes in v8:
time: 43.7 us; the launch traced here: 43.4 us
  blocking collectives  33 us (76%)
  Pallas kernels  3.88 us (9%)
  waiting for transfers between devices  3.69 us (8%)
  starting transfers between devices  1.61 us (4%)
  between operations  0.79 us (2%)
    all_to_all x2, blocking collectives, body(): got = lax.all_to_all(send, members, 0, 0, tiled=True)  33 us
    ppermute x1, waiting for transfers between devices, body(): came = lax.ppermute(state, ('hi', 'lo'), onward)  3.69 us
    ppermute x1, starting transfers between devices, body(): came = lax.ppermute(state, ('hi', 'lo'), onward)  1.61 us
    pallas_call x1, Pallas kernels, body(): call(bind(window_kernel, dims), [modes_shape, steps_shape, (groups, rows,...  1.16 us
    pallas_call x1, Pallas kernels, body(): call(bind(backward_kernel, dims), [(1, 5, depth, width_x, width_y)], [VME...  1.14 us
    pallas_call x1, Pallas kernels, body(): call(bind(first_kernel, dims), [state_shape, modes_shape, steps_shape, (c...  1.06 us
  transfers between devices with their start and end apart: 1, of which 1 were waited for; matrix products, arithmetic and copies ran while one was open for 0% of the time, Pallas kernels for 3%

profile of v8, /device:TPU:0, one launch (start us, length us, event | category | flops | bytes accessed | tf_op | source)
XLA Modules:
  0.0 43.4 jit_solution(1155963566832347589)
XLA Ops:
  0.0 0.0 copy-start.6
  0.0 0.0 copy-start.1
  0.0 0.0 copy-start.4
  0.0 0.0 copy-start.3
  0.0 0.0 copy-start
  0.0 0.0 copy-start.2
  0.0 0.0 copy-start.7
  0.8 0.0 copy-done.6
  0.8 0.3 copy-done.1
  1.1 0.0 copy-done.4
  1.2 0.0 copy-done.3
  1.2 0.5 %shard_map.92 = f32[16,88,128]{2,1,0:T(8,128)S(1)} custom-call(f32[1]{0:T(128)S(6)} %copy.16.step_ref, f32[2,128,128]{2,1,0:T(8,128)S(1)} %copy-done.3, f32[1,2,128,128]{3,2,1,0:T(8,128)S(1)} %copy-done.4, f32[1,5,2,128,128]{4,3,2,1,0:T(8,128)S(1)} %copy-done.1, bf16[2,128,128]{2,1,0:T(8,128)(2,1)S(1)} %copy-done.6, bf16[128,128]{1,0:T(8,128)(2,1)S(1)} %shard_map.91.blank_ref), custom_call_target="tpu_custom_call" | custom-call | tf_op jit(solution)/shard_map/pallas_call | solution.py:485
  1.7 18.5 %all_to_all.10.got_ref = f32[16,88,128]{2,1,0:T(8,128)S(1)} all-to-all(f32[16,88,128]{2,1,0:T(8,128)S(1)} %shard_map.92), channel_id=1, replica_groups=mesh['hi'=2,'lo'=4,'chip'=2,'core'=2] {'core','lo','chip'}, dimensions={0} | all-to-all | bytes 1441792 | tf_op jit(solution)/shard_map/all_to_all | solution.py:492
  20.2 0.0 copy-done
  20.2 0.0 copy-done.2
  20.2 0.0 copy-done.7
  20.2 1.1 %shard_map.93 = (f32[3,8,8,128]{3,2,1,0:T(8,128)S(1)}, f32[4,5,8,8,128]{4,3,2,1,0:T(8,128)S(1)}, f32[4,8,128]{2,1,0:T(8,128)S(1)}, f32[8,8,128]{2,1,0:T(8,128)S(1)}) custom-call(f32[16,88,128]{2,1,0:T(8,128)S(1)} %all_to_all.10.got_ref, bf16[256,256]{1,0:T(8,128)(2,1)S(1)} %copy-done, f32[128,128]{1,0:T(8,128)S(1)} %copy-done.2, f32[1,128]{1,0:T(1,128)S(1)} %copy-done.7), custom_call_target="tpu_custom_call" | custom-call | tf_op jit(solution)/shard_map/pallas_call | solution.py:494
  21.3 1.6 %collective-permute-start = (f32[3,8,8,128]{3,2,1,0:T(8,128)S(1)}, f32[3,8,8,128]{3,2,1,0:T(8,128)S(1)}, u32[]{:S(2)}, u32[]{:S(2)}) collective-permute-start(f32[3,8,8,128]{3,2,1,0:T(8,128)S(1)} %get-tuple-element.18), channel_id=1, source_target_pairs={{0,16},{4,20},{8,24},{12,28},{16,8},{20,12},{24,0},{28,4},{1,17},{... | collective-permute-start | bytes 294920 | tf_op jit(solution)/shard_map/ppermute | solution.py:501
  22.9 1.2 %shard_map.94 = (f32[4,5,8,8,128]{4,3,2,1,0:T(8,128)S(1)}, f32[4,8,128]{2,1,0:T(8,128)S(1)}, f32[16,80,128]{2,1,0:T(8,128)S(1)}, f32[17,8,8,128]{3,2,1,0:T(8,128)S(1)}, f32[3,17,8,8,128]{4,3,2,1,0:T(8,128)S(1)}) custom-call(f32[16,88,128]{2,1,0:T(8,128)S(1)} %all_to_all.10.got_ref, ...), custom_call_target="tpu_custom_call", output_to_operand_aliasing={{0}: (1, {}), {1}: (2, {})} | custom-call | tf_op jit(solution)/shard_map/pallas_call | solution.py:503
  24.1 3.7 %collective-permute-done.came_ref = f32[3,8,8,128]{3,2,1,0:T(8,128)S(1)} collective-permute-done((f32[3,8,8,128]{3,2,1,0:T(8,128)S(1)}, f32[3,8,8,128]{3,2,1,0:T(8,128)S(1)}, u32[]{:S(2)}, u32[]{:S(2)}) %collective-permute-start) | collective-permute-done | bytes 98336 | tf_op jit(solution)/shard_map/ppermute | solution.py:501
  27.8 0.0 copy-start.5
  27.8 14.5 %all_to_all.11.got_ref = f32[16,80,128]{2,1,0:T(8,128)S(1)} all-to-all(f32[16,80,128]{2,1,0:T(8,128)S(1)} %shard_map.95), channel_id=1, replica_groups=mesh['hi'=2,'lo'=4,'chip'=2,'core'=2] {'core','lo','chip'}, dimensions={0} | all-to-all | bytes 1310720 | tf_op jit(solution)/shard_map/all_to_all | solution.py:523
  42.3 0.0 copy-done.5
  42.3 1.1 %shard_map.96 = f32[1,5,2,128,128]{4,3,2,1,0:T(8,128)} custom-call(f32[16,80,128]{2,1,0:T(8,128)S(1)} %all_to_all.11.got_ref, bf16[256,256]{1,0:T(8,128)(2,1)S(1)} %copy-done.5), custom_call_target="tpu_custom_call" | custom-call | tf_op jit(solution)/shard_map/pallas_call | solution.py:524
  (2 shorter events, 0.0 us)
Async XLA Ops:
  0.0 0.8 %copy-start.6 = (bf16[2,128,128]{2,1,0:T(8,128)(2,1)S(1)}, bf16[2,128,128]{2,1,0:T(8,128)(2,1)}, u32[]{:S(2)}) copy-start(bf16[2,128,128]{2,1,0:T(8,128)(2,1)} %constant.10.clone.parts_ref) | copy-start | bytes 196612
  0.0 1.1 %copy-start.1 = (f32[1,5,2,128,128]{4,3,2,1,0:T(8,128)S(1)}, f32[1,5,2,128,128]{4,3,2,1,0:T(8,128)}, u32[]{:S(2)}) copy-start(f32[1,5,2,128,128]{4,3,2,1,0:T(8,128)} %forcing_ref.1) | copy-start | bytes 1966084
  0.0 1.2 %copy-start.4 = (f32[1,2,128,128]{3,2,1,0:T(8,128)S(1)}, f32[1,2,128,128]{3,2,1,0:T(8,128)}, u32[]{:S(2)}) copy-start(f32[1,2,128,128]{3,2,1,0:T(8,128)} %guess_ref.1) | copy-start | bytes 393220
  0.0 1.2 %copy-start.3 = (f32[2,128,128]{2,1,0:T(8,128)S(1)}, f32[2,128,128]{2,1,0:T(8,128)}, u32[]{:S(2)}) copy-start(f32[2,128,128]{2,1,0:T(8,128)} %init_ref.1) | copy-start | bytes 393220
  0.0 20.2 %copy-start = (bf16[256,256]{1,0:T(8,128)(2,1)S(1)}, bf16[256,256]{1,0:T(8,128)(2,1)}, u32[]{:S(2)}) copy-start(bf16[256,256]{1,0:T(8,128)(2,1)} %constant.11.clone.right_ref) | copy-start | bytes 393220
  0.0 20.2 %copy-start.2 = (f32[128,128]{1,0:T(8,128)S(1)}, f32[128,128]{1,0:T(8,128)}, u32[]{:S(2)}) copy-start(f32[128,128]{1,0:T(8,128)} %constant.13.clone.x_ref) | copy-start | bytes 196612
  0.0 20.2 %copy-start.7 = (f32[1,128]{1,0:T(1,128)S(1)}, f32[1,128]{1,0:T(1,128)}, u32[]{:S(2)}) copy-start(f32[1,128]{1,0:T(1,128)} %constant.14.clone.y_ref) | copy-start | bytes 1540
  21.3 6.5 %collective-permute-start = (f32[3,8,8,128]{3,2,1,0:T(8,128)S(1)}, f32[3,8,8,128]{3,2,1,0:T(8,128)S(1)}, u32[]{:S(2)}, u32[]{:S(2)}) collective-permute-start(f32[3,8,8,128]{3,2,1,0:T(8,128)S(1)} %get-tuple-element.18), channel_id=1, source_target_pairs={{0,16},{4,20},{8,24},{12,28},{16,8},{20,12},{24,0},{28,4},{1,17},{... | collective-permute-start | bytes 294920 | tf_op jit(solution)/shard_map/ppermute | solution.py:501
  27.8 14.5 %copy-start.5 = (bf16[256,256]{1,0:T(8,128)(2,1)S(1)}, bf16[256,256]{1,0:T(8,128)(2,1)}, u32[]{:S(2)}) copy-start(bf16[256,256]{1,0:T(8,128)(2,1)} %constant.12.clone.left_ref) | copy-start | bytes 393220

commit v9 on v8

--- a/solution.py
+++ b/solution.py
@@ -261,12 +261,12 @@
     return (device % cores * lo + j) * (space // cores) + device // cores, z % depth
 
 
-def to_modes(dims, got_ref, right_ref, modes_ref, steps_ref):
+def to_modes(dims, got_ref, right_ref, modes_ref, steps_ref, start_ref=None):
     depth, groups, per, lo, space, cores = dims
     base = 5 * depth * per + per // (lo // depth)
     count = depth * space
+    columns = []
     for j in range(lo):
-        columns = []
         for f in range(5):
             tiles = []
             for z in range(count):
@@ -274,14 +274,21 @@
                 row = (f * depth + d) * per
                 tiles.append(got_ref[device, row : row + per, :])
             columns += sine_list(tiles)
-        mixed = times_sine(jnp.concatenate(columns, axis=0), right_ref[...])
-        modes_ref[j] = mixed.reshape(5, count, per, mixed.shape[1])
         steps_ref[j] = jnp.broadcast_to(
             got_ref[source(dims, j, 0)[0], base : base + 1, :], steps_ref.shape[1:]
         )
-
-
-def initial_modes(dims, got_ref, right_ref):
+    if start_ref is not None:
+        columns += initial_modes(dims, got_ref)
+    mixed = times_sine(jnp.concatenate(columns, axis=0), right_ref[...])
+    size = 5 * count * per
+    for j in range(lo):
+        part = mixed[j * size : (j + 1) * size]
+        modes_ref[j] = part.reshape(5, count, per, mixed.shape[1])
+    if start_ref is not None:
+        start_ref[...] = mixed[lo * size :].reshape(count, per, mixed.shape[1])
+
+
+def initial_modes(dims, got_ref):
     depth, groups, per, lo, space, cores = dims
     pieces = lo // depth
     base = 5 * depth * per
@@ -294,8 +301,7 @@
             for i in range(first, first + pieces)
         ]
         tiles.append(jnp.concatenate(parts, axis=0))
-    mixed = times_sine(jnp.concatenate(sine_list(tiles), axis=0), right_ref[...])
-    return mixed.reshape(depth * space, per, mixed.shape[1])
+    return sine_list(tiles)
 
 
 def per_mode(dims, modes_ref, steps_ref, x_ref, y_ref):
@@ -334,8 +340,7 @@
 ):
     @pl.when(lax.axis_index("hi") == 0)
     def _():
-        to_modes(dims, got_ref, right_ref, modes_ref, steps_ref)
-        start_ref[...] = initial_modes(dims, got_ref, right_ref)
+        to_modes(dims, got_ref, right_ref, modes_ref, steps_ref, start_ref)
         for z, guesses, forced, scaled in per_mode(dims, modes_ref, steps_ref, x_ref, y_ref):
             state = march(guesses, forced, scaled, (start_ref[z],) * 3, False)
             for i in range(3):

time: 43.7 us -> 43.6 us (level)
  no operation moved by 1% of the time
where the time goes in v9:
time: 43.6 us; the launch traced here: 43.4 us
  blocking collectives  33 us (76%)
  Pallas kernels  3.85 us (9%)
  waiting for transfers between devices  3.66 us (8%)
  starting transfers between devices  1.64 us (4%)
  between operations  0.79 us (2%)
    all_to_all x2, blocking collectives, body(): got = lax.all_to_all(send, members, 0, 0, tiled=True)  33 us
    ppermute x1, waiting for transfers between devices, body(): came = lax.ppermute(state, ('hi', 'lo'), onward)  3.66 us
    ppermute x1, starting transfers between devices, body(): came = lax.ppermute(state, ('hi', 'lo'), onward)  1.64 us
    pallas_call x1, Pallas kernels, body(): call(bind(window_kernel, dims), [modes_shape, steps_shape, (groups, rows,...  1.16 us
    pallas_call x1, Pallas kernels, body(): call(bind(backward_kernel, dims), [(1, 5, depth, width_x, width_y)], [VME...  1.14 us
    pallas_call x1, Pallas kernels, body(): call(bind(first_kernel, dims), [state_shape, modes_shape, steps_shape, (c...  1.02 us
  transfers between devices with their start and end apart: 1, of which 1 were waited for; matrix products, arithmetic and copies ran while one was open for 0% of the time, Pallas kernels for 3%

profile of v9, /device:TPU:0, one launch (start us, length us, event | category | flops | bytes accessed | tf_op | source)
XLA Modules:
  0.0 43.4 jit_solution(18132347054353969731)
XLA Ops:
  0.0 0.0 copy-start.6
  0.0 0.0 copy-start.1
  0.0 0.0 copy-start.4
  0.0 0.0 copy-start.3
  0.0 0.0 copy-start
  0.0 0.0 copy-start.2
  0.0 0.0 copy-start.7
  0.8 0.0 copy-done.6
  0.8 0.3 copy-done.1
  1.1 0.0 copy-done.4
  1.2 0.0 copy-done.3
  1.2 0.5 %shard_map.92 = f32[16,88,128]{2,1,0:T(8,128)S(1)} custom-call(f32[1]{0:T(128)S(6)} %copy.16.step_ref, f32[2,128,128]{2,1,0:T(8,128)S(1)} %copy-done.3, f32[1,2,128,128]{3,2,1,0:T(8,128)S(1)} %copy-done.4, f32[1,5,2,128,128]{4,3,2,1,0:T(8,128)S(1)} %copy-done.1, bf16[2,128,128]{2,1,0:T(8,128)(2,1)S(1)} %copy-done.6, bf16[128,128]{1,0:T(8,128)(2,1)S(1)} %shard_map.91.blank_ref), custom_call_target="tpu_custom_call" | custom-call | tf_op jit(solution)/shard_map/pallas_call | solution.py:490
  1.7 18.5 %all_to_all.10.got_ref = f32[16,88,128]{2,1,0:T(8,128)S(1)} all-to-all(f32[16,88,128]{2,1,0:T(8,128)S(1)} %shard_map.92), channel_id=1, replica_groups=mesh['hi'=2,'lo'=4,'chip'=2,'core'=2] {'core','lo','chip'}, dimensions={0} | all-to-all | bytes 1441792 | tf_op jit(solution)/shard_map/all_to_all | solution.py:497
  20.2 0.0 copy-done
  20.2 0.0 copy-done.2
  20.2 0.0 copy-done.7
  20.2 1.0 %shard_map.93 = (f32[3,8,8,128]{3,2,1,0:T(8,128)S(1)}, f32[4,5,8,8,128]{4,3,2,1,0:T(8,128)S(1)}, f32[4,8,128]{2,1,0:T(8,128)S(1)}, f32[8,8,128]{2,1,0:T(8,128)S(1)}) custom-call(f32[16,88,128]{2,1,0:T(8,128)S(1)} %all_to_all.10.got_ref, bf16[256,256]{1,0:T(8,128)(2,1)S(1)} %copy-done, f32[128,128]{1,0:T(8,128)S(1)} %copy-done.2, f32[1,128]{1,0:T(1,128)S(1)} %copy-done.7), custom_call_target="tpu_custom_call" | custom-call | tf_op jit(solution)/shard_map/pallas_call | solution.py:499
  21.3 1.6 %collective-permute-start = (f32[3,8,8,128]{3,2,1,0:T(8,128)S(1)}, f32[3,8,8,128]{3,2,1,0:T(8,128)S(1)}, u32[]{:S(2)}, u32[]{:S(2)}) collective-permute-start(f32[3,8,8,128]{3,2,1,0:T(8,128)S(1)} %get-tuple-element.18), channel_id=1, source_target_pairs={{0,16},{4,20},{8,24},{12,28},{16,8},{20,12},{24,0},{28,4},{1,17},{... | collective-permute-start | bytes 294920 | tf_op jit(solution)/shard_map/ppermute | solution.py:506
  22.9 1.2 %shard_map.94 = (f32[4,5,8,8,128]{4,3,2,1,0:T(8,128)S(1)}, f32[4,8,128]{2,1,0:T(8,128)S(1)}, f32[16,80,128]{2,1,0:T(8,128)S(1)}, f32[17,8,8,128]{3,2,1,0:T(8,128)S(1)}, f32[3,17,8,8,128]{4,3,2,1,0:T(8,128)S(1)}) custom-call(f32[16,88,128]{2,1,0:T(8,128)S(1)} %all_to_all.10.got_ref, ...), custom_call_target="tpu_custom_call", output_to_operand_aliasing={{0}: (1, {}), {1}: (2, {})} | custom-call | tf_op jit(solution)/shard_map/pallas_call | solution.py:508
  24.1 3.7 %collective-permute-done.came_ref = f32[3,8,8,128]{3,2,1,0:T(8,128)S(1)} collective-permute-done((f32[3,8,8,128]{3,2,1,0:T(8,128)S(1)}, f32[3,8,8,128]{3,2,1,0:T(8,128)S(1)}, u32[]{:S(2)}, u32[]{:S(2)}) %collective-permute-start) | collective-permute-done | bytes 98336 | tf_op jit(solution)/shard_map/ppermute | solution.py:506
  27.7 0.0 copy-start.5
  27.7 14.5 %all_to_all.11.got_ref = f32[16,80,128]{2,1,0:T(8,128)S(1)} all-to-all(f32[16,80,128]{2,1,0:T(8,128)S(1)} %shard_map.95), channel_id=1, replica_groups=mesh['hi'=2,'lo'=4,'chip'=2,'core'=2] {'core','lo','chip'}, dimensions={0} | all-to-all | bytes 1310720 | tf_op jit(solution)/shard_map/all_to_all | solution.py:528
  42.3 0.0 copy-done.5
  42.3 1.1 %shard_map.96 = f32[1,5,2,128,128]{4,3,2,1,0:T(8,128)} custom-call(f32[16,80,128]{2,1,0:T(8,128)S(1)} %all_to_all.11.got_ref, bf16[256,256]{1,0:T(8,128)(2,1)S(1)} %copy-done.5), custom_call_target="tpu_custom_call" | custom-call | tf_op jit(solution)/shard_map/pallas_call | solution.py:529
  (2 shorter events, 0.0 us)
Async XLA Ops:
  0.0 0.8 %copy-start.6 = (bf16[2,128,128]{2,1,0:T(8,128)(2,1)S(1)}, bf16[2,128,128]{2,1,0:T(8,128)(2,1)}, u32[]{:S(2)}) copy-start(bf16[2,128,128]{2,1,0:T(8,128)(2,1)} %constant.10.clone.parts_ref) | copy-start | bytes 196612
  0.0 1.1 %copy-start.1 = (f32[1,5,2,128,128]{4,3,2,1,0:T(8,128)S(1)}, f32[1,5,2,128,128]{4,3,2,1,0:T(8,128)}, u32[]{:S(2)}) copy-start(f32[1,5,2,128,128]{4,3,2,1,0:T(8,128)} %forcing_ref.1) | copy-start | bytes 1966084
  0.0 1.2 %copy-start.4 = (f32[1,2,128,128]{3,2,1,0:T(8,128)S(1)}, f32[1,2,128,128]{3,2,1,0:T(8,128)}, u32[]{:S(2)}) copy-start(f32[1,2,128,128]{3,2,1,0:T(8,128)} %guess_ref.1) | copy-start | bytes 393220
  0.0 1.2 %copy-start.3 = (f32[2,128,128]{2,1,0:T(8,128)S(1)}, f32[2,128,128]{2,1,0:T(8,128)}, u32[]{:S(2)}) copy-start(f32[2,128,128]{2,1,0:T(8,128)} %init_ref.1) | copy-start | bytes 393220
  0.0 20.2 %copy-start = (bf16[256,256]{1,0:T(8,128)(2,1)S(1)}, bf16[256,256]{1,0:T(8,128)(2,1)}, u32[]{:S(2)}) copy-start(bf16[256,256]{1,0:T(8,128)(2,1)} %constant.11.clone.right_ref) | copy-start | bytes 393220
  0.0 20.2 %copy-start.2 = (f32[128,128]{1,0:T(8,128)S(1)}, f32[128,128]{1,0:T(8,128)}, u32[]{:S(2)}) copy-start(f32[128,128]{1,0:T(8,128)} %constant.13.clone.x_ref) | copy-start | bytes 196612
  0.0 20.2 %copy-start.7 = (f32[1,128]{1,0:T(1,128)S(1)}, f32[1,128]{1,0:T(1,128)}, u32[]{:S(2)}) copy-start(f32[1,128]{1,0:T(1,128)} %constant.14.clone.y_ref) | copy-start | bytes 1540
  21.3 6.5 %collective-permute-start = (f32[3,8,8,128]{3,2,1,0:T(8,128)S(1)}, f32[3,8,8,128]{3,2,1,0:T(8,128)S(1)}, u32[]{:S(2)}, u32[]{:S(2)}) collective-permute-start(f32[3,8,8,128]{3,2,1,0:T(8,128)S(1)} %get-tuple-element.18), channel_id=1, source_target_pairs={{0,16},{4,20},{8,24},{12,28},{16,8},{20,12},{24,0},{28,4},{1,17},{... | collective-permute-start | bytes 294920 | tf_op jit(solution)/shard_map/ppermute | solution.py:506
  27.7 14.5 %copy-start.5 = (bf16[256,256]{1,0:T(8,128)(2,1)S(1)}, bf16[256,256]{1,0:T(8,128)(2,1)}, u32[]{:S(2)}) copy-start(bf16[256,256]{1,0:T(8,128)(2,1)} %constant.12.clone.left_ref) | copy-start | bytes 393220
